TPU v7x, 32 devices: a whole 2x2x4 slice. The times are simulated.
32 devices in a mesh: gx: 8 (over z, x), gy: 4 (over y, core).
Axes of the slice: x: 2, y: 2, z: 4, core: 2. Of those that a mesh axis runs over, the one named last changes fastest.
Arguments:
- clm_block: int32 [262144], P(('gx', 'gy')), may hold values from 0 to 31, as said below
- clm_cell: int32 [262144], P(('gx', 'gy')), may hold values from 0 to 8191, as said below
- precip: float32 [262144], P(('gx', 'gy')), may hold values from 0.05 to 2
- evap_demand: float32 [262144], P(('gx', 'gy')), may hold values from 0.05 to 1
- root_share: float32 [10, 262144], P(None, ('gx', 'gy')), may hold values from 0.05 to 1
- sat_before: float32 [10, 262144], P(None, ('gx', 'gy')), may hold values from 0.2 to 1
- pressure: float32 [10, 256, 1024], P(None, 'gx', 'gy'), may hold values from -3 to 0.5
- conductivity: float32 [10, 256, 1024], P(None, 'gx', 'gy'), may hold values from 0.1 to 3
- porosity: float32 [10, 256, 1024], P(None, 'gx', 'gy'), may hold values from 0.25 to 0.5
- freeze_state: int32 [10, 256, 1024], P(None, 'gx', 'gy'), may hold values from 0 to 2
- land_mask: int32 [256, 1024], P('gx', 'gy'), may hold values 0 or 1
Outputs:
- new_pressure: float32 [10, 256, 1024], P(None, 'gx', 'gy')
- returned_sat: float32 [10, 262144], P(None, ('gx', 'gy'))
Inputs may be any that keep to these rules, and one draw needn't show every extreme that they name: Grid blocks are 32 x 256 columns, numbered with the second horizontal dimension fastest. Within one device's entries clm_block never falls; one device's entries name at most 384 columns of one block, and exactly that many for some blocks. `clm_cell`: together with clm_block, every grid column is named exactly once.
All inputs are finite; a program needn't handle non-finite values. No bound on the sum of `land_mask` on one device may be relied on, other than what follows from the above.
Results may differ from a plain program's by a relative error of at most 0.0002.
Values sent between devices are 32-bit elements; how exact they have to be, the bound alone decides.
No kernel may reach another device: no remote copies, remote signals or barrier semaphores. Data moves between devices by JAX's collectives and lax.ppermute only.
A program may use at most 64 MiB of HBM per device.

v0:
```python
import jax
import jax.numpy as jnp
from jax import lax
from jax.experimental import pallas as pl
from jax.experimental.pallas import tpu as pltpu
from jax.sharding import PartitionSpec as P

NEWTON = 2
SWEEPS = 4
OMEGA = 0.8
LANES = 128
ROWS = 8
HALO = 8
GROUPS = LANES // HALO


def params():
    return pltpu.CompilerParams(vmem_limit_bytes=48 * 2**20)


def saturation(field):
    dryness = jnp.maximum(-field, 0.0)
    return lax.rsqrt(1.0 + dryness * dryness)


def frozen_factor(freeze_state):
    return jnp.where(freeze_state == 0, 1.0, jnp.where(freeze_state == 1, 0.2, 0.02)).astype(
        jnp.float32
    )


def window_tiles(capacity):
    return capacity // LANES


def dispatch_kernel(layers, devices, capacity):
    chunks = window_tiles(capacity)
    fields = layers + 1

    def kernel(starts, block, cell, precip, evap, root, sat, out, packed):
        columns = root.shape[1]
        rows_of = 4 * LANES

        def flux(tile, carry):
            span = pl.ds(pl.multiple_of(tile * LANES, LANES), LANES)
            s = sat[:, span]
            w = root[:, span] * s * s
            total = 0.25 + jnp.sum(w, axis=0, keepdims=True)
            uptake = w * (evap[pl.ds(tile, 1), :] / total)
            top = s[0:1]
            rain = precip[pl.ds(tile, 1), :] * (1.0 - top * top * top)
            packed[0:1, span] = rain - uptake[0:1]
            packed[1:layers, span] = -uptake[1:]
            packed[layers:fields, span] = cell[pl.ds(tile, 1), :].astype(jnp.float32)
            return carry

        lax.fori_loop(0, columns // LANES, flux, 0, unroll=8)
        lane = lax.broadcasted_iota(jnp.int32, (1, LANES), 1)

        def window(owner, carry):
            start = starts[owner]
            count = starts[owner + 1] - start
            base = pl.multiple_of((start // LANES) * LANES, LANES)
            shift = start % LANES
            near = lane < LANES - shift
            turned = [
                pltpu.roll(packed[:, pl.ds(base + t * LANES, LANES)], LANES - shift, 1)
                for t in range(chunks + 1)
            ]
            for t in range(chunks):
                moved = jnp.where(near, turned[t], turned[t + 1])
                row = (owner * chunks + t) * fields
                held = t * LANES + lane < count
                out[pl.ds(row, layers), :] = moved[0:layers]
                out[pl.ds(row + layers, 1), :] = jnp.where(held, moved[layers:fields], -1.0)
            return carry

        lax.fori_loop(0, devices, window, 0, unroll=4)

    return kernel


def dispatch(starts, block, cell, precip, evap, root, sat, devices, capacity):
    layers, columns = root.shape
    fields = layers + 1
    rows = devices * window_tiles(capacity) * fields
    vmem = pl.BlockSpec(memory_space=pltpu.VMEM)
    fold = (columns // LANES, LANES)
    return pl.pallas_call(
        dispatch_kernel(layers, devices, capacity),
        out_shape=jax.ShapeDtypeStruct((rows, LANES), jnp.float32),
        in_specs=[pl.BlockSpec(memory_space=pltpu.SMEM)] + [vmem] * 6,
        out_specs=vmem,
        scratch_shapes=[pltpu.VMEM((2 * ROWS, columns + capacity + LANES), jnp.float32)],
        compiler_params=params(),
        name="dispatch",
    )(
        starts,
        block.reshape(fold),
        cell.reshape(fold),
        precip.reshape(fold),
        evap.reshape(fold),
        root,
        sat,
    )


def scatter_kernel(layers, cells_x, cells_y, batch):
    fields = layers + 1
    half = layers * cells_x

    def kernel(incoming, mask, out, low, high, total, spread):
        chunks = incoming.shape[0] // fields
        total[...] = jnp.zeros_like(total)
        row_x = lax.broadcasted_iota(jnp.int32, (cells_x, LANES), 0)
        row_y = lax.broadcasted_iota(jnp.int32, (cells_y, LANES), 0)

        def step(i, carry):
            onehots = []
            for b in range(batch):
                first = (i * batch + b) * fields
                cell = incoming[pl.ds(first + layers, 1), :].astype(jnp.int32)
                x = cell // cells_y
                y = cell - x * cells_y
                x = jnp.where(cell < 0, -1, x)
                onehots.append((row_y == y).astype(jnp.float32).astype(jnp.bfloat16))
                here = row_x == x
                values = incoming[pl.ds(first, layers), :]
                big = values.astype(jnp.bfloat16).astype(jnp.float32)
                small = values - big
                span = slice(b * LANES, (b + 1) * LANES)
                for k in range(layers):
                    rows = slice(k * cells_x, (k + 1) * cells_x)
                    spread[rows, span] = jnp.where(here, big[k : k + 1], 0.0).astype(jnp.bfloat16)
                    rows = slice(half + k * cells_x, half + (k + 1) * cells_x)
                    spread[rows, span] = jnp.where(here, small[k : k + 1], 0.0).astype(
                        jnp.bfloat16
                    )
            onehot = jnp.concatenate(onehots, axis=1)
            total[...] += lax.dot_general(
                spread[...],
                onehot,
                (((1,), (1,)), ((), ())),
                preferred_element_type=jnp.float32,
            )
            return carry

        lax.fori_loop(0, chunks // batch, step, 0)
        land = mask[...].astype(jnp.float32)
        for k in range(layers):
            rows = slice(k * cells_x, (k + 1) * cells_x)
            lower = slice(half + k * cells_x, half + (k + 1) * cells_x)
            source = (total[rows, :] + total[lower, :]) * land
            out[k] = source
            low[k] = source[:HALO]
            high[k] = source[cells_x - HALO :]

    return kernel


def scatter(incoming, mask, layers, cells_x, cells_y):
    chunks = incoming.shape[0] // (layers + 1)
    batch = max(b for b in (8, 6, 4, 3, 2, 1) if chunks % b == 0)
    strip = jax.ShapeDtypeStruct((layers, HALO, cells_y), jnp.float32)
    vmem = pl.BlockSpec(memory_space=pltpu.VMEM)
    return pl.pallas_call(
        scatter_kernel(layers, cells_x, cells_y, batch),
        out_shape=(jax.ShapeDtypeStruct((layers, cells_x, cells_y), jnp.float32), strip, strip),
        in_specs=[vmem, vmem],
        out_specs=(vmem, vmem, vmem),
        scratch_shapes=[
            pltpu.VMEM((2 * layers * cells_x, cells_y), jnp.float32),
            pltpu.VMEM((2 * layers * cells_x, batch * LANES), jnp.bfloat16),
        ],
        compiler_params=params(),
        name="scatter",
    )(incoming, mask)


def both_ways(low_end, high_end, axis):
    count = lax.axis_size(axis)
    forward = [(i, i + 1) for i in range(count - 1)]
    backward = [(target, source) for source, target in forward]
    return lax.ppermute(high_end, axis, forward), lax.ppermute(low_end, axis, backward)


def packed_rows(layers, cells_x):
    tiles = layers * (cells_x + 2 * HALO) // ROWS
    return -(-tiles // GROUPS) * ROWS


def tile_places(layers, cells_x):
    tiles = (cells_x + 2 * HALO) // ROWS
    for index in range(layers * tiles):
        yield index // tiles, index % tiles, index // GROUPS, index % GROUPS


def pack_kernel(layers, cells_x, cells_y):
    lane_of = lambda: lax.broadcasted_iota(jnp.int32, (ROWS, LANES), 1)

    def kernel(middle, below, above, left, right):
        fields = middle.shape[0]
        lane = lane_of()
        last = cells_x // ROWS + 1

        def column(f, k, t, cols):
            if t == 0:
                return below[f, k, :, cols]
            if t == last:
                return above[f, k, :, cols]
            return middle[f, k, (t - 1) * ROWS : t * ROWS, cols]

        for f in range(fields):
            for out, cols, offset in (
                (left, slice(0, LANES), 0),
                (right, slice(cells_y - LANES, cells_y), LANES - HALO),
            ):
                held = {}
                for k, t, place, group in tile_places(layers, cells_x):
                    tile = column(f, k, t, cols)
                    turn = (group * HALO - offset) % LANES
                    tile = pltpu.roll(tile, turn, 1) if turn else tile
                    if group == 0:
                        held[place] = tile
                    else:
                        here = (lane >= group * HALO) & (lane < (group + 1) * HALO)
                        held[place] = jnp.where(here, tile, held[place])
                for place, tile in held.items():
                    out[f, place * ROWS : (place + 1) * ROWS, :] = tile

    return kernel


def pack(middle, below, above):
    fields, layers, cells_x, cells_y = middle.shape
    out = jax.ShapeDtypeStruct((fields, packed_rows(layers, cells_x), LANES), jnp.float32)
    vmem = pl.BlockSpec(memory_space=pltpu.VMEM)
    return pl.pallas_call(
        pack_kernel(layers, cells_x, cells_y),
        out_shape=(out, out),
        in_specs=[vmem] * 3,
        out_specs=(vmem, vmem),
        compiler_params=params(),
        name="pack",
    )(middle, below, above)


def prepare_kernel(conductivity, freeze, porosity, pressure, out, low, high):
    cells_x = out.shape[2]
    perm = conductivity[...] * frozen_factor(freeze[...])
    for f, value in enumerate((perm, porosity[...], pressure[...])):
        out[f] = value
        low[f] = value[:, :HALO]
        high[f] = value[:, cells_x - HALO :]


def prepare(conductivity, freeze, porosity, pressure):
    layers, cells_x, cells_y = pressure.shape
    strip = jax.ShapeDtypeStruct((3, layers, HALO, cells_y), jnp.float32)
    vmem = pl.BlockSpec(memory_space=pltpu.VMEM)
    return pl.pallas_call(
        prepare_kernel,
        out_shape=(jax.ShapeDtypeStruct((3, layers, cells_x, cells_y), jnp.float32), strip, strip),
        in_specs=[vmem] * 4,
        out_specs=(vmem,) * 3,
        compiler_params=params(),
        name="prepare",
    )(conductivity, freeze, porosity, pressure)


def gather_slots(incoming, table, reply, layers, cells_x, cells_y):
    fields = layers + 1
    chunks = incoming.shape[0] // fields
    sub = lax.broadcasted_iota(jnp.int32, (ROWS, LANES), 0)
    across = cells_y // LANES
    groups = cells_x // ROWS * across

    def body(c, carry):
        cell = incoming[pl.ds(c * fields + layers, 1), :].astype(jnp.int32)
        cell = jnp.broadcast_to(jnp.maximum(cell, 0), (ROWS, LANES))
        x = cell // cells_y
        y = cell - x * cells_y
        lane = y % LANES
        group = (x // ROWS) * across + y // LANES
        wanted = x % ROWS == sub
        rows = []
        for k in range(layers):
            value = jnp.zeros((ROWS, LANES), jnp.float32)
            for g in range(groups):
                first = HALO + g // across * ROWS
                tile = table[k, first : first + ROWS, g % across * LANES : (g % across + 1) * LANES]
                found = jnp.take_along_axis(tile, lane, axis=1, mode="promise_in_bounds")
                value = jnp.where(group == g, found, value)
            value = jnp.where(wanted, value, 0.0)
            rows.append(jnp.sum(value, axis=0, keepdims=True))
        reply[pl.ds(c * layers, layers), :] = jnp.concatenate(rows, axis=0)
        return carry

    lax.fori_loop(0, chunks, body, 0, unroll=2)


def newton_kernel(layers, cells_x, cells_y):
    high_x = cells_x + 2 * HALO
    wide = cells_y + LANES

    def up(v):
        return pltpu.roll(v, high_x - 1, 0)

    def down(v):
        return pltpu.roll(v, 1, 0)

    def right(v):
        return pltpu.roll(v, wide - 1, 1)

    def left(v):
        return pltpu.roll(v, 1, 1)

    def kernel(
        fixed, fixed_low, fixed_high, fixed_left, fixed_right,
        src, src_low, src_high, src_left, src_right, incoming,
        new_pressure, reply,
        perm, poro, source, pres, stored,
        tx, ty, tz, rel, gz, flow,
        ax, bx, ay, by, az, bz, resid, update,
    ):
        lane = lax.broadcasted_iota(jnp.int32, (ROWS, LANES), 1)
        last = cells_x // ROWS + 1

        def widen(dest, field, middle, low, high, side_left, side_right):
            dest[:, HALO : HALO + cells_x, :cells_y] = middle[field]
            dest[:, :HALO, :cells_y] = low[field]
            dest[:, HALO + cells_x :, :cells_y] = high[field]
            for k, t, place, group in tile_places(layers, cells_x):
                rows = slice(place * ROWS, (place + 1) * ROWS)
                turn = (LANES - HALO - group * HALO) % LANES
                a = side_left[field, rows, :]
                a = pltpu.roll(a, turn, 1) if turn else a
                turn = (-group * HALO) % LANES
                b = side_right[field, rows, :]
                b = pltpu.roll(b, turn, 1) if turn else b
                tile = jnp.where(lane < HALO, b, jnp.where(lane >= LANES - HALO, a, 0.0))
                dest[k, t * ROWS : (t + 1) * ROWS, cells_y:] = tile

        widen(perm, 0, fixed, fixed_low, fixed_high, fixed_left, fixed_right)
        widen(poro, 1, fixed, fixed_low, fixed_high, fixed_left, fixed_right)
        widen(pres, 2, fixed, fixed_low, fixed_high, fixed_left, fixed_right)
        widen(source, 0, src, src_low, src_high, src_left, src_right)

        def face(a, b):
            joined = a + b
            return a * b / jnp.where(joined > 0.0, joined, 1.0)

        def still(k, carry):
            a = perm[k]
            tx[k] = face(a, up(a))
            ty[k] = face(a, right(a))
            tz[k] = face(a, perm[jnp.minimum(k + 1, layers - 1)])
            stored[k] = saturation(pres[k])
            return carry

        lax.fori_loop(0, layers, still, 0)

        for newton_step in range(NEWTON):

            def relative(k, carry):
                s = saturation(pres[k])
                rel[k] = s * s * s
                return carry

            lax.fori_loop(0, layers, relative, 0)

            def vertical(k, carry):
                r = rel[k]
                below = jnp.minimum(k + 1, layers - 1)
                g = tz[k] * (r + rel[below])
                inside = k < layers - 1
                g = jnp.where(inside, g, 0.0)
                gz[k + 1] = g
                drained = perm[k] * r
                flow[k + 1] = jnp.where(inside, g * (pres[k] - pres[below] + 1.0), drained)
                return carry

            gz[0] = jnp.zeros((high_x, wide), jnp.float32)
            flow[0] = jnp.zeros((high_x, wide), jnp.float32)
            lax.fori_loop(0, layers, vertical, 0)

            def linear(k, carry):
                p = pres[k]
                r = rel[k]
                gx = tx[k] * (r + up(r))
                gy = ty[k] * (r + right(r))
                fx = gx * (p - up(p))
                fy = gy * (p - right(p))
                gxd = down(gx)
                gyd = left(gy)
                s = saturation(p)
                porous = poro[k]
                residual = porous * (s - stored[k])
                residual = residual + (fx - down(fx)) + (fy - left(fy))
                residual = residual + (flow[k + 1] - flow[k]) - source[k]
                gzd = gz[k]
                gzu = gz[k + 1]
                diagonal = porous * (jnp.maximum(-p, 0.0) * r)
                diagonal = diagonal + (gx + gxd) + (gy + gyd) + (gzu + gzd)
                diagonal = jnp.where(diagonal > 0.0, diagonal, 1.0)
                scale = OMEGA / diagonal
                ax[k] = scale * gx
                bx[k] = scale * gxd
                ay[k] = scale * gy
                by[k] = scale * gyd
                az[k] = scale * gzu
                bz[k] = scale * gzd
                residual = scale * residual
                resid[k] = residual
                update[0, k] = -residual
                return carry

            lax.fori_loop(0, layers, linear, 0)

            for sweep in range(SWEEPS - 1):
                old = sweep % 2
                new = 1 - old

                def smooth(k, carry):
                    u = update[old, k]
                    v = (1.0 - OMEGA) * u - resid[k]
                    v = v + ax[k] * up(u) + bx[k] * down(u)
                    v = v + ay[k] * right(u) + by[k] * left(u)
                    v = v + az[k] * update[old, jnp.minimum(k + 1, layers - 1)]
                    v = v + bz[k] * update[old, jnp.maximum(k - 1, 0)]
                    update[new, k] = v
                    if sweep == SWEEPS - 2:
                        pres[k] = pres[k] + v
                    return carry

                lax.fori_loop(0, layers, smooth, 0)

        def finish(k, carry):
            p = pres[k, HALO : HALO + cells_x, :cells_y]
            new_pressure[k] = p
            rel[k, HALO : HALO + cells_x, :cells_y] = saturation(p)
            return carry

        lax.fori_loop(0, layers, finish, 0)
        gather_slots(incoming, rel, reply, layers, cells_x, cells_y)

    return kernel


def newton(fixed, source, incoming, layers, cells_x, cells_y):
    chunks = incoming.shape[0] // (layers + 1)
    high_x, wide = cells_x + 2 * HALO, cells_y + LANES
    field = pltpu.VMEM((layers, high_x, wide), jnp.float32)
    taller = pltpu.VMEM((layers + 1, high_x, wide), jnp.float32)
    vmem = pl.BlockSpec(memory_space=pltpu.VMEM)
    return pl.pallas_call(
        newton_kernel(layers, cells_x, cells_y),
        out_shape=(
            jax.ShapeDtypeStruct((layers, cells_x, cells_y), jnp.float32),
            jax.ShapeDtypeStruct((chunks * layers, LANES), jnp.float32),
        ),
        in_specs=[vmem] * 11,
        out_specs=(vmem, vmem),
        scratch_shapes=[field] * 5
        + [field] * 4
        + [taller] * 2
        + [field] * 7
        + [pltpu.VMEM((2, layers, high_x, wide), jnp.float32)],
        compiler_params=params(),
        name="newton",
    )(*fixed, *source, incoming)


def combine_kernel(layers, devices, capacity):
    chunks = window_tiles(capacity)

    def kernel(starts, answer, out, wide):
        lane = lax.broadcasted_iota(jnp.int32, (1, LANES), 1)

        def window(owner, carry):
            start = starts[owner]
            base = pl.multiple_of((start // LANES) * LANES, LANES)
            shift = start % LANES
            before = lane < shift
            row = owner * chunks * layers
            kept = wide[0:layers, pl.ds(base, LANES)]
            for t in range(chunks):
                turned = pltpu.roll(answer[pl.ds(row + t * layers, layers), :], shift, 1)
                wide[0:layers, pl.ds(base + t * LANES, LANES)] = jnp.where(before, kept, turned)
                kept = turned
            wide[0:layers, pl.ds(base + chunks * LANES, LANES)] = kept
            return carry

        lax.fori_loop(0, devices, window, 0)
        out[...] = wide[0:layers, : out.shape[1]]

    return kernel


def combine(starts, answer, layers, columns, devices, capacity):
    vmem = pl.BlockSpec(memory_space=pltpu.VMEM)
    return pl.pallas_call(
        combine_kernel(layers, devices, capacity),
        out_shape=jax.ShapeDtypeStruct((layers, columns), jnp.float32),
        in_specs=[pl.BlockSpec(memory_space=pltpu.SMEM), vmem],
        out_specs=vmem,
        scratch_shapes=[pltpu.VMEM((2 * ROWS, columns + capacity + LANES), jnp.float32)],
        compiler_params=params(),
        name="combine",
    )(starts, answer)


def on_device(
    clm_block,
    clm_cell,
    precip,
    evap_demand,
    root_share,
    sat_before,
    pressure,
    conductivity,
    porosity,
    freeze_state,
    land_mask,
):
    axes = ("gx", "gy")
    layers, columns = root_share.shape
    devices = lax.axis_size("gx") * lax.axis_size("gy")
    cells_x, cells_y = pressure.shape[1], pressure.shape[2]
    per_pair = columns // devices
    capacity = -(-(per_pair + per_pair // 2) // LANES) * LANES
    owners = jnp.arange(devices + 1, dtype=jnp.int32)
    starts = jnp.sum((clm_block[None, :] < owners[:, None]).astype(jnp.int32), axis=1)

    outgoing = dispatch(
        starts, clm_block, clm_cell, precip, evap_demand, root_share, sat_before, devices, capacity
    )
    flat = lax.all_to_all(outgoing.reshape(-1), axes, split_axis=0, concat_axis=0, tiled=True)
    incoming = flat.reshape(outgoing.shape)

    fixed, low, high = prepare(conductivity, freeze_state, porosity, pressure)
    below, above = both_ways(low, high, "gx")
    to_left, to_right = pack(fixed, below, above)
    side_left, side_right = both_ways(to_left, to_right, "gy")
    fixed = (fixed, below, above, side_left, side_right)

    source, low, high = scatter(incoming, land_mask, layers, cells_x, cells_y)
    below, above = both_ways(low, high, "gx")
    source, below, above = source[None], below[None], above[None]
    to_left, to_right = pack(source, below, above)
    side_left, side_right = both_ways(to_left, to_right, "gy")
    source = (source, below, above, side_left, side_right)

    new_pressure, reply = newton(fixed, source, incoming, layers, cells_x, cells_y)
    flat = lax.all_to_all(reply.reshape(-1), axes, split_axis=0, concat_axis=0, tiled=True)
    returned = combine(starts, flat.reshape(reply.shape), layers, columns, devices, capacity)
    return (new_pressure, returned)


def solution(mesh):
    columns = P(("gx", "gy"))
    layered = P(None, ("gx", "gy"))
    grid = P(None, "gx", "gy")
    return jax.shard_map(
        on_device,
        mesh=mesh,
        in_specs=(columns,) * 4 + (layered,) * 2 + (grid,) * 4 + (P("gx", "gy"),),
        out_specs=(grid, layered),
        check_vma=False,
    )
```

profile of v0, /device:TPU:0, one launch (start us, length us, event | category | flops | bytes accessed | tf_op | source)
XLA Modules:
  0.0 109.5 jit_solution(13805756916680458055)
XLA Ops:
  0.6 1.0 convert_reduce_fusion.starts
  1.6 0.0 copy-start
  1.6 1.0 copy-done
  2.7 0.0 copy-start.1
  2.7 1.0 copy-done.1
  3.7 0.0 copy-start.6
  3.7 0.8 copy-done.6
  4.5 0.0 copy-start.7
  4.5 0.8 copy-done.7
  5.2 0.0 copy-start.8
  5.2 0.8 copy-done.8
  6.0 0.0 copy-start.9
  6.0 0.8 copy-done.9
  6.8 0.0 copy-start.2
  6.8 0.0 copy-start.3
  6.8 0.0 copy-start.4
  6.8 0.0 copy-start.5
  6.8 2.7 %dispatch.1 = f32[1056,128]{1,0:T(8,128)} custom-call(s32[33]{0:T(128)S(1)} %convert_reduce_fusion.starts, s32[64,128]{1,0:T(8,128)S(1)} %bitcast.21, s32[64,128]{1,0:T(8,128)S(1)} %bitcast.22, f32[64,128]{1,0:T(8,128)S(1)} %bitcast.23, f32[64,128]{1,0:T(8,128)S(1)} %bitcast.24, f32[10,8192]{1,0:T(8,128)S(1)} %copy-done, f32[10,8192]{1,0:T(8,128)S(1)} %copy-done.1), custom_call_target="tpu_custom_call" | custom-call | tf_op jit(solution)/shard_map/dispatch/pallas_call | solution.py:89
  9.5 7.3 %all-to-all-start = ((f32[32,4224,1]{1,2,0:T(1,128)}), f32[32,4224,1]{1,2,0:T(1,128)S(1)}, u32[]{:S(2)}, u32[]{:S(2)}) async-start(f32[32,4224,1]{1,2,0:T(1,128)} %bitcast.4), calls=%async_computation | async-start | bytes 1081344 | tf_op jit(solution)/shard_map/all_to_all | solution.py:538
  16.8 0.0 copy-done.2
  16.8 0.0 copy-done.3
  16.8 0.0 copy-done.4
  16.9 0.0 copy-done.5
  16.9 0.1 prepare.1
  17.0 3.7 %collective-permute-start = (f32[3,10,8,256]{3,2,1,0:T(8,128)S(1)}, f32[3,10,8,256]{3,2,1,0:T(8,128)S(1)}, u32[]{:S(2)}, u32[]{:S(2)}) collective-permute-start(f32[3,10,8,256]{3,2,1,0:T(8,128)S(1)} %get-tuple-element.15), channel_id=1, source_target_pairs={{0,4},{4,8},{8,12},{12,16},{16,20},{20,24},{24,28},{1,5},{5,9},{9,... | collective-permute-start | bytes 737288 | tf_op jit(solution)/shard_map/ppermute | solution.py:184
  20.7 1.3 %collective-permute-start.1 = (f32[3,10,8,256]{3,2,1,0:T(8,128)S(1)}, f32[3,10,8,256]{3,2,1,0:T(8,128)S(1)}, u32[]{:S(2)}, u32[]{:S(2)}) collective-permute-start(f32[3,10,8,256]{3,2,1,0:T(8,128)S(1)} %get-tuple-element.16), channel_id=1, source_target_pairs={{4,0},{8,4},{12,8},{16,12},{20,16},{24,20},{28,24},{5,1},{9,5},{13... | collective-permute-start | bytes 737288 | tf_op jit(solution)/shard_map/ppermute | solution.py:184
  22.0 10.7 %all-to-all-done = f32[32,4224,1]{1,2,0:T(1,128)S(1)} async-done(((f32[32,4224,1]{1,2,0:T(1,128)}), f32[32,4224,1]{1,2,0:T(1,128)S(1)}, u32[]{:S(2)}, u32[]{:S(2)}) %all-to-all-start) | async-done | bytes 540704 | tf_op jit(solution)/shard_map/all_to_all | solution.py:538
  32.7 0.0 copy-done.10
  32.7 7.6 %scatter.1 = (f32[10,32,256]{2,1,0:T(8,128)S(1)}, f32[10,8,256]{2,1,0:T(8,128)S(1)}, f32[10,8,256]{2,1,0:T(8,128)S(1)}) custom-call(f32[1056,128]{1,0:T(8,128)S(1)} %bitcast.11, s32[32,256]{1,0:T(8,128)S(1)} %copy-done.10), custom_call_target="tpu_custom_call" | custom-call | tf_op jit(solution)/shard_map/scatter/pallas_call | solution.py:166
  40.4 3.3 %collective-permute-start.4 = (f32[10,8,256]{2,1,0:T(8,128)S(1)}, f32[10,8,256]{2,1,0:T(8,128)S(1)}, u32[]{:S(2)}, u32[]{:S(2)}) collective-permute-start(f32[10,8,256]{2,1,0:T(8,128)S(1)} %get-tuple-element.20), channel_id=1, source_target_pairs={{0,4},{4,8},{8,12},{12,16},{16,20},{20,24},{24,28},{1,5},{5,9},{9,... | collective-permute-start | bytes 245768 | tf_op jit(solution)/shard_map/ppermute | solution.py:184
  43.6 1.3 %collective-permute-start.5 = (f32[10,8,256]{2,1,0:T(8,128)S(1)}, f32[10,8,256]{2,1,0:T(8,128)S(1)}, u32[]{:S(2)}, u32[]{:S(2)}) collective-permute-start(f32[10,8,256]{2,1,0:T(8,128)S(1)} %get-tuple-element.21), channel_id=1, source_target_pairs={{4,0},{8,4},{12,8},{16,12},{20,16},{24,20},{28,24},{5,1},{9,5},{13... | collective-permute-start | bytes 245768 | tf_op jit(solution)/shard_map/ppermute | solution.py:184
  44.9 0.0 collective-permute-done.below.fixed_low
  45.0 0.0 collective-permute-done.1.above.fixed_high
  45.0 0.4 pack.2
  45.4 1.5 %collective-permute-start.2 = (f32[3,32,128]{2,1,0:T(8,128)S(1)}, f32[3,32,128]{2,1,0:T(8,128)S(1)}, u32[]{:S(2)}, u32[]{:S(2)}) collective-permute-start(f32[3,32,128]{2,1,0:T(8,128)S(1)} %get-tuple-element.17), channel_id=1, source_target_pairs={{0,1},{1,2},{2,3},{4,5},{5,6},{6,7},{8,9},{9,10},{10,11},{12,13},{... | collective-permute-start | bytes 147464 | tf_op jit(solution)/shard_map/ppermute | solution.py:184
  46.9 1.3 %collective-permute-start.3 = (f32[3,32,128]{2,1,0:T(8,128)S(1)}, f32[3,32,128]{2,1,0:T(8,128)S(1)}, u32[]{:S(2)}, u32[]{:S(2)}) collective-permute-start(f32[3,32,128]{2,1,0:T(8,128)S(1)} %get-tuple-element.18), channel_id=1, source_target_pairs={{1,0},{2,1},{3,2},{5,4},{6,5},{7,6},{9,8},{10,9},{11,10},{13,12},{... | collective-permute-start | bytes 147464 | tf_op jit(solution)/shard_map/ppermute | solution.py:184
  48.2 0.0 collective-permute-done.4
  48.2 1.8 %collective-permute-done.5 = f32[10,8,256]{2,1,0:T(8,128)S(1)} collective-permute-done((f32[10,8,256]{2,1,0:T(8,128)S(1)}, f32[10,8,256]{2,1,0:T(8,128)S(1)}, u32[]{:S(2)}, u32[]{:S(2)}) %collective-permute-start.5) | collective-permute-done | bytes 81952 | tf_op jit(solution)/shard_map/ppermute | solution.py:184
  50.0 0.2 pack.3
  50.2 2.3 %collective-permute-start.6 = (f32[1,32,128]{2,1,0:T(8,128)S(1)}, f32[1,32,128]{2,1,0:T(8,128)S(1)}, u32[]{:S(2)}, u32[]{:S(2)}) collective-permute-start(f32[1,32,128]{2,1,0:T(8,128)S(1)} %get-tuple-element.22), channel_id=1, source_target_pairs={{0,1},{1,2},{2,3},{4,5},{5,6},{6,7},{8,9},{9,10},{10,11},{12,13},{... | collective-permute-start | bytes 49160 | tf_op jit(solution)/shard_map/ppermute | solution.py:184
  52.5 1.3 %collective-permute-start.7 = (f32[1,32,128]{2,1,0:T(8,128)S(1)}, f32[1,32,128]{2,1,0:T(8,128)S(1)}, u32[]{:S(2)}, u32[]{:S(2)}) collective-permute-start(f32[1,32,128]{2,1,0:T(8,128)S(1)} %get-tuple-element.23), channel_id=1, source_target_pairs={{1,0},{2,1},{3,2},{5,4},{6,5},{7,6},{9,8},{10,9},{11,10},{13,12},{... | collective-permute-start | bytes 49160 | tf_op jit(solution)/shard_map/ppermute | solution.py:184
  53.8 0.0 collective-permute-done.2.fixed_left
  53.8 0.0 collective-permute-done.3.fixed_right
  53.8 0.0 collective-permute-done.6.src_left
  53.8 3.0 %collective-permute-done.7.src_right = f32[1,32,128]{2,1,0:T(8,128)S(1)} collective-permute-done((f32[1,32,128]{2,1,0:T(8,128)S(1)}, f32[1,32,128]{2,1,0:T(8,128)S(1)}, u32[]{:S(2)}, u32[]{:S(2)}) %collective-permute-start.7) | collective-permute-done | bytes 16416 | tf_op jit(solution)/shard_map/ppermute | solution.py:184
  56.8 28.0 %newton.1 = (f32[10,32,256]{2,1,0:T(8,128)}, f32[960,128]{1,0:T(8,128)S(1)}) custom-call(f32[3,10,32,256]{3,2,1,0:T(8,128)S(1)} %get-tuple-element.14.middle.fixed, f32[3,10,8,256]{3,2,1,0:T(8,128)S(1)} %collective-permute-done.below.fixed_low, f32[3,10,8,256]{3,2,1,0:T(8,128)S(1)} %collective-permute-done.1.above.fixed_high, ...), custom_call_target="tpu_custom_call" | custom-call | tf_op jit(solution)/shard_map/newton/pallas_call | solution.py:456
  84.8 20.9 %all_to_all.18 = f32[32,3840,1]{1,2,0:T(1,128)S(1)} all-to-all(f32[32,3840,1]{1,2,0:T(1,128)S(1)} %bitcast.16), channel_id=1, replica_groups=mesh['gx'=8,'gy'=4] {'gx','gy'}, dimensions={0} | all-to-all | bytes 983040 | tf_op jit(solution)/shard_map/all_to_all | solution.py:555
  105.7 3.8 %combine.1 = f32[10,8192]{1,0:T(8,128)} custom-call(s32[33]{0:T(128)S(1)} %convert_reduce_fusion.starts, f32[960,128]{1,0:T(8,128)S(1)} %bitcast.13), custom_call_target="tpu_custom_call" | custom-call | tf_op jit(solution)/shard_map/combine/pallas_call | solution.py:502
  (1 shorter events, 0.0 us)
Async XLA Ops:
  1.6 1.1 copy-start
  2.7 1.0 copy-start.1
  3.7 0.8 copy-start.6
  4.5 0.8 copy-start.7
  5.2 0.8 copy-start.8
  6.0 0.8 copy-start.9
  6.8 10.1 %copy-start.2 = (f32[10,32,256]{2,1,0:T(8,128)S(1)}, f32[10,32,256]{2,1,0:T(8,128)}, u32[]{:S(2)}) copy-start(f32[10,32,256]{2,1,0:T(8,128)} %conductivity.1) | copy-start | bytes 983044
  6.8 10.1 %copy-start.3 = (s32[10,32,256]{2,1,0:T(8,128)S(1)}, s32[10,32,256]{2,1,0:T(8,128)}, u32[]{:S(2)}) copy-start(s32[10,32,256]{2,1,0:T(8,128)} %freeze.1) | copy-start | bytes 983044
  6.8 10.1 %copy-start.4 = (f32[10,32,256]{2,1,0:T(8,128)S(1)}, f32[10,32,256]{2,1,0:T(8,128)}, u32[]{:S(2)}) copy-start(f32[10,32,256]{2,1,0:T(8,128)} %porosity.1) | copy-start | bytes 983044
  6.8 10.1 %copy-start.5 = (f32[10,32,256]{2,1,0:T(8,128)S(1)}, f32[10,32,256]{2,1,0:T(8,128)}, u32[]{:S(2)}) copy-start(f32[10,32,256]{2,1,0:T(8,128)} %pressure.1) | copy-start | bytes 983044
  9.5 23.3 %copy-start.10 = (s32[32,256]{1,0:T(8,128)S(1)}, s32[32,256]{1,0:T(8,128)}, u32[]{:S(2)}) copy-start(s32[32,256]{1,0:T(8,128)} %mask.1) | copy-start | bytes 98308
  9.5 23.2 %all-to-all-start = ((f32[32,4224,1]{1,2,0:T(1,128)}), f32[32,4224,1]{1,2,0:T(1,128)S(1)}, u32[]{:S(2)}, u32[]{:S(2)}) async-start(f32[32,4224,1]{1,2,0:T(1,128)} %bitcast.4), calls=%async_computation | async-start | bytes 1081344 | tf_op jit(solution)/shard_map/all_to_all | solution.py:538
  17.0 28.0 %collective-permute-start = (f32[3,10,8,256]{3,2,1,0:T(8,128)S(1)}, f32[3,10,8,256]{3,2,1,0:T(8,128)S(1)}, u32[]{:S(2)}, u32[]{:S(2)}) collective-permute-start(f32[3,10,8,256]{3,2,1,0:T(8,128)S(1)} %get-tuple-element.15), channel_id=1, source_target_pairs={{0,4},{4,8},{8,12},{12,16},{16,20},{20,24},{24,28},{1,5},{5,9},{9,... | collective-permute-start | bytes 737288 | tf_op jit(solution)/shard_map/ppermute | solution.py:184
  20.7 24.3 %collective-permute-start.1 = (f32[3,10,8,256]{3,2,1,0:T(8,128)S(1)}, f32[3,10,8,256]{3,2,1,0:T(8,128)S(1)}, u32[]{:S(2)}, u32[]{:S(2)}) collective-permute-start(f32[3,10,8,256]{3,2,1,0:T(8,128)S(1)} %get-tuple-element.16), channel_id=1, source_target_pairs={{4,0},{8,4},{12,8},{16,12},{20,16},{24,20},{28,24},{5,1},{9,5},{13... | collective-permute-start | bytes 737288 | tf_op jit(solution)/shard_map/ppermute | solution.py:184
  40.4 7.8 %collective-permute-start.4 = (f32[10,8,256]{2,1,0:T(8,128)S(1)}, f32[10,8,256]{2,1,0:T(8,128)S(1)}, u32[]{:S(2)}, u32[]{:S(2)}) collective-permute-start(f32[10,8,256]{2,1,0:T(8,128)S(1)} %get-tuple-element.20), channel_id=1, source_target_pairs={{0,4},{4,8},{8,12},{12,16},{16,20},{20,24},{24,28},{1,5},{5,9},{9,... | collective-permute-start | bytes 245768 | tf_op jit(solution)/shard_map/ppermute | solution.py:184
  43.6 6.3 %collective-permute-start.5 = (f32[10,8,256]{2,1,0:T(8,128)S(1)}, f32[10,8,256]{2,1,0:T(8,128)S(1)}, u32[]{:S(2)}, u32[]{:S(2)}) collective-permute-start(f32[10,8,256]{2,1,0:T(8,128)S(1)} %get-tuple-element.21), channel_id=1, source_target_pairs={{4,0},{8,4},{12,8},{16,12},{20,16},{24,20},{28,24},{5,1},{9,5},{13... | collective-permute-start | bytes 245768 | tf_op jit(solution)/shard_map/ppermute | solution.py:184
  45.4 8.4 %collective-permute-start.2 = (f32[3,32,128]{2,1,0:T(8,128)S(1)}, f32[3,32,128]{2,1,0:T(8,128)S(1)}, u32[]{:S(2)}, u32[]{:S(2)}) collective-permute-start(f32[3,32,128]{2,1,0:T(8,128)S(1)} %get-tuple-element.17), channel_id=1, source_target_pairs={{0,1},{1,2},{2,3},{4,5},{5,6},{6,7},{8,9},{9,10},{10,11},{12,13},{... | collective-permute-start | bytes 147464 | tf_op jit(solution)/shard_map/ppermute | solution.py:184
  46.9 6.9 %collective-permute-start.3 = (f32[3,32,128]{2,1,0:T(8,128)S(1)}, f32[3,32,128]{2,1,0:T(8,128)S(1)}, u32[]{:S(2)}, u32[]{:S(2)}) collective-permute-start(f32[3,32,128]{2,1,0:T(8,128)S(1)} %get-tuple-element.18), channel_id=1, source_target_pairs={{1,0},{2,1},{3,2},{5,4},{6,5},{7,6},{9,8},{10,9},{11,10},{13,12},{... | collective-permute-start | bytes 147464 | tf_op jit(solution)/shard_map/ppermute | solution.py:184
  50.2 3.7 %collective-permute-start.6 = (f32[1,32,128]{2,1,0:T(8,128)S(1)}, f32[1,32,128]{2,1,0:T(8,128)S(1)}, u32[]{:S(2)}, u32[]{:S(2)}) collective-permute-start(f32[1,32,128]{2,1,0:T(8,128)S(1)} %get-tuple-element.22), channel_id=1, source_target_pairs={{0,1},{1,2},{2,3},{4,5},{5,6},{6,7},{8,9},{9,10},{10,11},{12,13},{... | collective-permute-start | bytes 49160 | tf_op jit(solution)/shard_map/ppermute | solution.py:184
  52.5 4.3 %collective-permute-start.7 = (f32[1,32,128]{2,1,0:T(8,128)S(1)}, f32[1,32,128]{2,1,0:T(8,128)S(1)}, u32[]{:S(2)}, u32[]{:S(2)}) collective-permute-start(f32[1,32,128]{2,1,0:T(8,128)S(1)} %get-tuple-element.23), channel_id=1, source_target_pairs={{1,0},{2,1},{3,2},{5,4},{6,5},{7,6},{9,8},{10,9},{11,10},{13,12},{... | collective-permute-start | bytes 49160 | tf_op jit(solution)/shard_map/ppermute | solution.py:184
where the time goes:
time: 110 us
  Pallas kernels  42.8 us (39%)
  starting transfers between devices  23.2 us (21%)
  blocking collectives  20.9 us (19%)
  waiting for transfers between devices  15.5 us (14%)
  local copies, waits for them, and re-layouts  5.13 us (5%)
    pallas_call x1, Pallas kernels, newton(): pl.pallas_call(newton_kernel(layers, cells_x, cells_y), out_shape=(jax.Sh...  28 us
    all_to_all x1, blocking collectives, on_device(): lax.all_to_all(reply.reshape(-1), axes, split_axis=0, concat_axis=0, tile...  20.9 us
    all_to_all x1, waiting for transfers between devices, on_device(): lax.all_to_all(outgoing.reshape(-1), axes, split_axis=0, concat_axis=0, t...  10.7 us
    ppermute x4, starting transfers between devices, both_ways(): lax.ppermute(high_end, axis, forward)  10.7 us
    pallas_call x1, Pallas kernels, scatter(): pl.pallas_call(scatter_kernel(layers, cells_x, cells_y, batch), out_shape...  7.62 us
    all_to_all x1, starting transfers between devices, on_device(): lax.all_to_all(outgoing.reshape(-1), axes, split_axis=0, concat_axis=0, t...  7.33 us
    ppermute x4, starting transfers between devices, both_ways(): lax.ppermute(low_end, axis, backward)  5.17 us
    unnamed x22, local copies, waits for them, and re-layouts  5.13 us
  transfers between devices with their start and end apart: 9, of which 3 were waited for; matrix products, arithmetic and copies ran while one was open for 0% of the time, Pallas kernels for 8%

commit v1 on v0

--- a/solution.py
+++ b/solution.py
@@ -33,13 +33,61 @@
     return capacity // LANES
 
 
+def scalar_rows(count):
+    return -(-count // LANES)
+
+
+def to_scalars(column, staged, scalars):
+    count = column.shape[0]
+    for j in range(scalar_rows(count)):
+        part = column[j * LANES : (j + 1) * LANES]
+        shape = (part.shape[0], LANES)
+        own = lax.broadcasted_iota(jnp.int32, shape, 0) == lax.broadcasted_iota(jnp.int32, shape, 1)
+        staged[j : j + 1, :] = jnp.sum(jnp.where(own, part, 0), axis=0, keepdims=True)
+    pltpu.sync_copy(staged, scalars)
+
+
+def scalar_at(scalars, index):
+    if scalars.shape[0] == 1:
+        return scalars[0, index]
+    return scalars[index // LANES, index % LANES]
+
+
 def dispatch_kernel(layers, devices, capacity):
     chunks = window_tiles(capacity)
     fields = layers + 1
-
-    def kernel(starts, block, cell, precip, evap, root, sat, out, packed):
+    bounds = -(-(devices + 1) // ROWS) * ROWS
+
+    def kernel(
+        block_hbm, cell_hbm, precip_hbm, evap_hbm, root_hbm, sat_hbm,
+        out, starts,
+        packed, block, cell, precip, evap, root, sat, staged, sems,
+    ):
         columns = root.shape[1]
-        rows_of = 4 * LANES
+        copies = [
+            pltpu.make_async_copy(source, target, sems.at[i])
+            for i, (source, target) in enumerate(
+                (
+                    (block_hbm, block),
+                    (root_hbm, root),
+                    (sat_hbm, sat),
+                    (cell_hbm, cell),
+                    (precip_hbm, precip),
+                    (evap_hbm, evap),
+                )
+            )
+        ]
+        for copy in copies:
+            copy.start()
+        copies[0].wait()
+        owner_row = lax.broadcasted_iota(jnp.int32, (bounds, LANES), 0)
+        before = jnp.zeros((bounds, LANES), jnp.int32)
+        for r in range(columns // LANES):
+            before = before + (block[r : r + 1, :] < owner_row).astype(jnp.int32)
+        before = jnp.sum(before.astype(jnp.float32), axis=1, keepdims=True)
+        to_scalars(before.astype(jnp.int32), staged, starts)
+        for copy in copies[1:]:
+            copy.wait()
 
         def flux(tile, carry):
             span = pl.ds(pl.multiple_of(tile * LANES, LANES), LANES)
@@ -54,12 +102,12 @@
             packed[layers:fields, span] = cell[pl.ds(tile, 1), :].astype(jnp.float32)
             return carry
 
-        lax.fori_loop(0, columns // LANES, flux, 0, unroll=8)
+        lax.fori_loop(0, columns // LANES, flux, 0, unroll=16)
         lane = lax.broadcasted_iota(jnp.int32, (1, LANES), 1)
 
         def window(owner, carry):
-            start = starts[owner]
-            count = starts[owner + 1] - start
+            start = scalar_at(starts, owner)
+            count = scalar_at(starts, owner + 1) - start
             base = pl.multiple_of((start // LANES) * LANES, LANES)
             shift = start % LANES
             near = lane < LANES - shift
@@ -80,28 +128,46 @@
     return kernel
 
 
-def dispatch(starts, block, cell, precip, evap, root, sat, devices, capacity):
+def dispatch(block, cell, precip, evap, root, sat, devices, capacity):
     layers, columns = root.shape
     fields = layers + 1
     rows = devices * window_tiles(capacity) * fields
+    bounds = scalar_rows(-(-(devices + 1) // ROWS) * ROWS)
     vmem = pl.BlockSpec(memory_space=pltpu.VMEM)
     fold = (columns // LANES, LANES)
     return pl.pallas_call(
         dispatch_kernel(layers, devices, capacity),
-        out_shape=jax.ShapeDtypeStruct((rows, LANES), jnp.float32),
-        in_specs=[pl.BlockSpec(memory_space=pltpu.SMEM)] + [vmem] * 6,
-        out_specs=vmem,
-        scratch_shapes=[pltpu.VMEM((2 * ROWS, columns + capacity + LANES), jnp.float32)],
+        out_shape=(
+            jax.ShapeDtypeStruct((rows, LANES), jnp.float32),
+            jax.ShapeDtypeStruct((bounds, LANES), jnp.int32),
+        ),
+        in_specs=[pl.BlockSpec(memory_space=pltpu.HBM)] * 6,
+        out_specs=(vmem, pl.BlockSpec(memory_space=pltpu.SMEM)),
+        scratch_shapes=[
+            pltpu.VMEM((2 * ROWS, columns + capacity + LANES), jnp.float32),
+            pltpu.VMEM(fold, jnp.int32),
+            pltpu.VMEM(fold, jnp.int32),
+            pltpu.VMEM(fold, jnp.float32),
+            pltpu.VMEM(fold, jnp.float32),
+            pltpu.VMEM(root.shape, jnp.float32),
+            pltpu.VMEM(root.shape, jnp.float32),
+            pltpu.VMEM((bounds, LANES), jnp.int32),
+            pltpu.SemaphoreType.DMA((6,)),
+        ],
         compiler_params=params(),
         name="dispatch",
     )(
-        starts,
-        block.reshape(fold),
-        cell.reshape(fold),
-        precip.reshape(fold),
-        evap.reshape(fold),
-        root,
-        sat,
+        *(
+            pltpu.with_memory_space_constraint(a, pltpu.HBM)
+            for a in (
+                block.reshape(fold),
+                cell.reshape(fold),
+                precip.reshape(fold),
+                evap.reshape(fold),
+                root,
+                sat,
+            )
+        )
     )
 
 
@@ -109,8 +175,19 @@
     fields = layers + 1
     half = layers * cells_x
 
-    def kernel(incoming, mask, out, low, high, total, spread):
+    def kernel(incoming, mask, out, low, high, order, total, spread, staged, used):
         chunks = incoming.shape[0] // fields
+        first_cells = incoming[pl.ds(layers, chunks, stride=fields), :][:, 0:1]
+        to_scalars((first_cells >= 0.0).astype(jnp.int32), staged, used)
+
+        def listed(c, filled):
+            holds = scalar_at(used, c)
+            order[jnp.where(holds > 0, filled, chunks - 1 - (c - filled))] = c
+            return filled + holds
+
+        filled = lax.fori_loop(0, chunks, listed, 0, unroll=8)
+        batches = (filled + batch - 1) // batch
+        order[chunks] = filled
         total[...] = jnp.zeros_like(total)
         row_x = lax.broadcasted_iota(jnp.int32, (cells_x, LANES), 0)
         row_y = lax.broadcasted_iota(jnp.int32, (cells_y, LANES), 0)
@@ -118,7 +195,7 @@
         def step(i, carry):
             onehots = []
             for b in range(batch):
-                first = (i * batch + b) * fields
+                first = order[i * batch + b] * fields
                 cell = incoming[pl.ds(first + layers, 1), :].astype(jnp.int32)
                 x = cell // cells_y
                 y = cell - x * cells_y
@@ -145,7 +222,7 @@
             )
             return carry
 
-        lax.fori_loop(0, chunks // batch, step, 0)
+        lax.fori_loop(0, batches, step, 0)
         land = mask[...].astype(jnp.float32)
         for k in range(layers):
             rows = slice(k * cells_x, (k + 1) * cells_x)
@@ -165,12 +242,19 @@
     vmem = pl.BlockSpec(memory_space=pltpu.VMEM)
     return pl.pallas_call(
         scatter_kernel(layers, cells_x, cells_y, batch),
-        out_shape=(jax.ShapeDtypeStruct((layers, cells_x, cells_y), jnp.float32), strip, strip),
+        out_shape=(
+            jax.ShapeDtypeStruct((layers, cells_x, cells_y), jnp.float32),
+            strip,
+            strip,
+            jax.ShapeDtypeStruct((chunks + 1,), jnp.int32),
+        ),
         in_specs=[vmem, vmem],
-        out_specs=(vmem, vmem, vmem),
+        out_specs=(vmem, vmem, vmem, pl.BlockSpec(memory_space=pltpu.SMEM)),
         scratch_shapes=[
             pltpu.VMEM((2 * layers * cells_x, cells_y), jnp.float32),
             pltpu.VMEM((2 * layers * cells_x, batch * LANES), jnp.bfloat16),
+            pltpu.VMEM((scalar_rows(chunks), LANES), jnp.int32),
+            pltpu.SMEM((scalar_rows(chunks), LANES), jnp.int32),
         ],
         compiler_params=params(),
         name="scatter",
@@ -268,14 +352,14 @@
     )(conductivity, freeze, porosity, pressure)
 
 
-def gather_slots(incoming, table, reply, layers, cells_x, cells_y):
+def gather_slots(order, incoming, table, reply, layers, cells_x, cells_y):
     fields = layers + 1
     chunks = incoming.shape[0] // fields
     sub = lax.broadcasted_iota(jnp.int32, (ROWS, LANES), 0)
     across = cells_y // LANES
     groups = cells_x // ROWS * across
 
-    def body(c, carry):
+    def one(c):
         cell = incoming[pl.ds(c * fields + layers, 1), :].astype(jnp.int32)
         cell = jnp.broadcast_to(jnp.maximum(cell, 0), (ROWS, LANES))
         x = cell // cells_y
@@ -294,9 +378,15 @@
             value = jnp.where(wanted, value, 0.0)
             rows.append(jnp.sum(value, axis=0, keepdims=True))
         reply[pl.ds(c * layers, layers), :] = jnp.concatenate(rows, axis=0)
+
+    together = max(b for b in (4, 3, 2, 1) if chunks % b == 0)
+
+    def body(i, carry):
+        for b in range(together):
+            one(order[i * together + b])
         return carry
 
-    lax.fori_loop(0, chunks, body, 0, unroll=2)
+    lax.fori_loop(0, (order[chunks] + together - 1) // together, body, 0)
 
 
 def newton_kernel(layers, cells_x, cells_y):
@@ -315,9 +405,13 @@
     def left(v):
         return pltpu.roll(v, 1, 1)
 
+    def each_layer(do):
+        for k in range(layers):
+            do(k)
+
     def kernel(
         fixed, fixed_low, fixed_high, fixed_left, fixed_right,
-        src, src_low, src_high, src_left, src_right, incoming,
+        src, src_low, src_high, src_left, src_right, incoming, order,
         new_pressure, reply,
         perm, poro, source, pres, stored,
         tx, ty, tz, rel, gz, flow,
@@ -350,41 +444,39 @@
             joined = a + b
             return a * b / jnp.where(joined > 0.0, joined, 1.0)
 
-        def still(k, carry):
+        def still(k):
             a = perm[k]
             tx[k] = face(a, up(a))
             ty[k] = face(a, right(a))
-            tz[k] = face(a, perm[jnp.minimum(k + 1, layers - 1)])
+            tz[k] = face(a, perm[min(k + 1, layers - 1)])
             stored[k] = saturation(pres[k])
-            return carry
-
-        lax.fori_loop(0, layers, still, 0)
+
+        each_layer(still)
 
         for newton_step in range(NEWTON):
 
-            def relative(k, carry):
+            def relative(k):
                 s = saturation(pres[k])
                 rel[k] = s * s * s
-                return carry
-
-            lax.fori_loop(0, layers, relative, 0)
-
-            def vertical(k, carry):
+
+            each_layer(relative)
+
+            def vertical(k):
                 r = rel[k]
-                below = jnp.minimum(k + 1, layers - 1)
+                below = min(k + 1, layers - 1)
                 g = tz[k] * (r + rel[below])
-                inside = k < layers - 1
-                g = jnp.where(inside, g, 0.0)
-                gz[k + 1] = g
-                drained = perm[k] * r
-                flow[k + 1] = jnp.where(inside, g * (pres[k] - pres[below] + 1.0), drained)
-                return carry
+                if k < layers - 1:
+                    gz[k + 1] = g
+                    flow[k + 1] = g * (pres[k] - pres[below] + 1.0)
+                else:
+                    gz[k + 1] = jnp.zeros_like(g)
+                    flow[k + 1] = perm[k] * r
 
             gz[0] = jnp.zeros((high_x, wide), jnp.float32)
             flow[0] = jnp.zeros((high_x, wide), jnp.float32)
-            lax.fori_loop(0, layers, vertical, 0)
-
-            def linear(k, carry):
+            each_layer(vertical)
+
+            def linear(k):
                 p = pres[k]
                 r = rel[k]
                 gx = tx[k] * (r + up(r))
@@ -413,41 +505,38 @@
                 residual = scale * residual
                 resid[k] = residual
                 update[0, k] = -residual
-                return carry
-
-            lax.fori_loop(0, layers, linear, 0)
+
+            each_layer(linear)
 
             for sweep in range(SWEEPS - 1):
                 old = sweep % 2
                 new = 1 - old
 
-                def smooth(k, carry):
+                def smooth(k):
                     u = update[old, k]
                     v = (1.0 - OMEGA) * u - resid[k]
                     v = v + ax[k] * up(u) + bx[k] * down(u)
                     v = v + ay[k] * right(u) + by[k] * left(u)
-                    v = v + az[k] * update[old, jnp.minimum(k + 1, layers - 1)]
-                    v = v + bz[k] * update[old, jnp.maximum(k - 1, 0)]
+                    v = v + az[k] * update[old, min(k + 1, layers - 1)]
+                    v = v + bz[k] * update[old, max(k - 1, 0)]
                     update[new, k] = v
                     if sweep == SWEEPS - 2:
                         pres[k] = pres[k] + v
-                    return carry
-
-                lax.fori_loop(0, layers, smooth, 0)
-
-        def finish(k, carry):
+
+                each_layer(smooth)
+
+        def finish(k):
             p = pres[k, HALO : HALO + cells_x, :cells_y]
             new_pressure[k] = p
             rel[k, HALO : HALO + cells_x, :cells_y] = saturation(p)
-            return carry
-
-        lax.fori_loop(0, layers, finish, 0)
-        gather_slots(incoming, rel, reply, layers, cells_x, cells_y)
+
+        each_layer(finish)
+        gather_slots(order, incoming, rel, reply, layers, cells_x, cells_y)
 
     return kernel
 
 
-def newton(fixed, source, incoming, layers, cells_x, cells_y):
+def newton(fixed, source, incoming, order, layers, cells_x, cells_y):
     chunks = incoming.shape[0] // (layers + 1)
     high_x, wide = cells_x + 2 * HALO, cells_y + LANES
     field = pltpu.VMEM((layers, high_x, wide), jnp.float32)
@@ -459,7 +548,7 @@
             jax.ShapeDtypeStruct((layers, cells_x, cells_y), jnp.float32),
             jax.ShapeDtypeStruct((chunks * layers, LANES), jnp.float32),
         ),
-        in_specs=[vmem] * 11,
+        in_specs=[vmem] * 11 + [pl.BlockSpec(memory_space=pltpu.SMEM)],
         out_specs=(vmem, vmem),
         scratch_shapes=[field] * 5
         + [field] * 4
@@ -468,7 +557,7 @@
         + [pltpu.VMEM((2, layers, high_x, wide), jnp.float32)],
         compiler_params=params(),
         name="newton",
-    )(*fixed, *source, incoming)
+    )(*fixed, *source, incoming, order)
 
 
 def combine_kernel(layers, devices, capacity):
@@ -478,7 +567,7 @@
         lane = lax.broadcasted_iota(jnp.int32, (1, LANES), 1)
 
         def window(owner, carry):
-            start = starts[owner]
+            start = scalar_at(starts, owner)
             base = pl.multiple_of((start // LANES) * LANES, LANES)
             shift = start % LANES
             before = lane < shift
@@ -491,7 +580,7 @@
             wide[0:layers, pl.ds(base + chunks * LANES, LANES)] = kept
             return carry
 
-        lax.fori_loop(0, devices, window, 0)
+        lax.fori_loop(0, devices, window, 0, unroll=4)
         out[...] = wide[0:layers, : out.shape[1]]
 
     return kernel
@@ -529,11 +618,8 @@
     cells_x, cells_y = pressure.shape[1], pressure.shape[2]
     per_pair = columns // devices
     capacity = -(-(per_pair + per_pair // 2) // LANES) * LANES
-    owners = jnp.arange(devices + 1, dtype=jnp.int32)
-    starts = jnp.sum((clm_block[None, :] < owners[:, None]).astype(jnp.int32), axis=1)
-
-    outgoing = dispatch(
-        starts, clm_block, clm_cell, precip, evap_demand, root_share, sat_before, devices, capacity
+    outgoing, starts = dispatch(
+        clm_block, clm_cell, precip, evap_demand, root_share, sat_before, devices, capacity
     )
     flat = lax.all_to_all(outgoing.reshape(-1), axes, split_axis=0, concat_axis=0, tiled=True)
     incoming = flat.reshape(outgoing.shape)
@@ -544,14 +630,14 @@
     side_left, side_right = both_ways(to_left, to_right, "gy")
     fixed = (fixed, below, above, side_left, side_right)
 
-    source, low, high = scatter(incoming, land_mask, layers, cells_x, cells_y)
+    source, low, high, order = scatter(incoming, land_mask, layers, cells_x, cells_y)
     below, above = both_ways(low, high, "gx")
     source, below, above = source[None], below[None], above[None]
     to_left, to_right = pack(source, below, above)
     side_left, side_right = both_ways(to_left, to_right, "gy")
     source = (source, below, above, side_left, side_right)
 
-    new_pressure, reply = newton(fixed, source, incoming, layers, cells_x, cells_y)
+    new_pressure, reply = newton(fixed, source, incoming, order, layers, cells_x, cells_y)
     flat = lax.all_to_all(reply.reshape(-1), axes, split_axis=0, concat_axis=0, tiled=True)
     returned = combine(starts, flat.reshape(reply.shape), layers, columns, devices, capacity)
     return (new_pressure, returned)

time: 110 us -> 89.8 us (0.82)
  Pallas kernels: 42.8 us -> 28.7 us
  local copies, waits for them, and re-layouts: 5.13 us -> 0.03 us
    pallas_call x1, Pallas kernels: 28 us -> 15.4 us  [newton(): pl.pallas_call(newton_kernel(layers, cells_x, cells_y), out_shape=(jax.Sh...]
    unnamed x22 -> x10, local copies, waits for them, and re-layouts: 5.13 us -> 0.03 us
    pallas_call x1, Pallas kernels: 3.77 us -> 2.19 us  [combine(): pl.pallas_call(combine_kernel(layers, devices, capacity), out_shape=jax.S...]
where the time goes in v1:
time: 89.8 us; the launch traced here: 89.3 us
  Pallas kernels  28.7 us (32%)
  starting transfers between devices  23.2 us (26%)
  blocking collectives  20.9 us (23%)
  waiting for transfers between devices  15.5 us (17%)
    all_to_all x1, blocking collectives, on_device(): lax.all_to_all(reply.reshape(-1), axes, split_axis=0, concat_axis=0, tile...  20.9 us
    pallas_call x1, Pallas kernels, newton(): pl.pallas_call(newton_kernel(layers, cells_x, cells_y), out_shape=(jax.Sh...  15.4 us
    all_to_all x1, waiting for transfers between devices, on_device(): lax.all_to_all(outgoing.reshape(-1), axes, split_axis=0, concat_axis=0, t...  10.7 us
    ppermute x4, starting transfers between devices, both_ways(): lax.ppermute(high_end, axis, forward)  10.7 us
    all_to_all x1, starting transfers between devices, on_device(): lax.all_to_all(outgoing.reshape(-1), axes, split_axis=0, concat_axis=0, t...  7.33 us
    pallas_call x1, Pallas kernels, scatter(): pl.pallas_call(scatter_kernel(layers, cells_x, cells_y, batch), out_shape...  6.59 us
    ppermute x4, starting transfers between devices, both_ways(): lax.ppermute(low_end, axis, backward)  5.17 us
    ppermute x4, waiting for transfers between devices, both_ways(): lax.ppermute(low_end, axis, backward)  4.79 us
  transfers between devices with their start and end apart: 9, of which 3 were waited for; matrix products, arithmetic and copies ran while one was open for 0% of the time, Pallas kernels for 8%

profile of v1, /device:TPU:0, one launch (start us, length us, event | category | flops | bytes accessed | tf_op | source)
XLA Modules:
  0.0 89.3 jit_solution(8744077748831337121)
XLA Ops:
  0.6 0.0 copy-start.3
  0.6 3.8 %dispatch.1 = (f32[1056,128]{1,0:T(8,128)}, s32[1,128]{1,0:T(1,128)S(1)}) custom-call(s32[64,128]{1,0:T(8,128)} %bitcast.21, s32[64,128]{1,0:T(8,128)} %bitcast.22, f32[64,128]{1,0:T(8,128)} %bitcast.23, f32[64,128]{1,0:T(8,128)} %bitcast.24, f32[10,8192]{1,0:T(8,128)} %root_hbm.1, f32[10,8192]{1,0:T(8,128)} %sat_hbm.1), custom_call_target="tpu_custom_call" | custom-call | tf_op jit(solution)/shard_map/dispatch/pallas_call | solution.py:138
  4.4 0.0 copy-start
  4.4 0.0 copy-start.1
  4.5 0.0 copy-start.2
  4.5 7.3 %all-to-all-start = ((f32[32,4224,1]{1,2,0:T(1,128)}), f32[32,4224,1]{1,2,0:T(1,128)S(1)}, u32[]{:S(2)}, u32[]{:S(2)}) async-start(f32[32,4224,1]{1,2,0:T(1,128)} %bitcast.4), calls=%async_computation | async-start | bytes 1081344 | tf_op jit(solution)/shard_map/all_to_all | solution.py:624
  11.8 0.0 copy-done.3
  11.8 0.0 copy-done
  11.8 0.0 copy-done.1
  11.8 0.0 copy-done.2
  11.8 0.0 copy-start.4
  11.9 0.1 prepare.1
  12.0 3.7 %collective-permute-start = (f32[3,10,8,256]{3,2,1,0:T(8,128)S(1)}, f32[3,10,8,256]{3,2,1,0:T(8,128)S(1)}, u32[]{:S(2)}, u32[]{:S(2)}) collective-permute-start(f32[3,10,8,256]{3,2,1,0:T(8,128)S(1)} %get-tuple-element.18), channel_id=1, source_target_pairs={{0,4},{4,8},{8,12},{12,16},{16,20},{20,24},{24,28},{1,5},{5,9},{9,... | collective-permute-start | bytes 737288 | tf_op jit(solution)/shard_map/ppermute | solution.py:268
  15.7 1.3 %collective-permute-start.1 = (f32[3,10,8,256]{3,2,1,0:T(8,128)S(1)}, f32[3,10,8,256]{3,2,1,0:T(8,128)S(1)}, u32[]{:S(2)}, u32[]{:S(2)}) collective-permute-start(f32[3,10,8,256]{3,2,1,0:T(8,128)S(1)} %get-tuple-element.19), channel_id=1, source_target_pairs={{4,0},{8,4},{12,8},{16,12},{20,16},{24,20},{28,24},{5,1},{9,5},{13... | collective-permute-start | bytes 737288 | tf_op jit(solution)/shard_map/ppermute | solution.py:268
  17.0 10.7 %all-to-all-done = f32[32,4224,1]{1,2,0:T(1,128)S(1)} async-done(((f32[32,4224,1]{1,2,0:T(1,128)}), f32[32,4224,1]{1,2,0:T(1,128)S(1)}, u32[]{:S(2)}, u32[]{:S(2)}) %all-to-all-start) | async-done | bytes 540704 | tf_op jit(solution)/shard_map/all_to_all | solution.py:624
  27.7 0.0 copy-done.4
  27.7 6.6 %scatter.1 = (f32[10,32,256]{2,1,0:T(8,128)S(1)}, f32[10,8,256]{2,1,0:T(8,128)S(1)}, f32[10,8,256]{2,1,0:T(8,128)S(1)}, s32[97]{0:T(128)S(1)}) custom-call(f32[1056,128]{1,0:T(8,128)S(1)} %bitcast.11, s32[32,256]{1,0:T(8,128)S(1)} %copy-done.4), custom_call_target="tpu_custom_call" | custom-call | tf_op jit(solution)/shard_map/scatter/pallas_call | solution.py:243
  34.3 3.3 %collective-permute-start.4 = (f32[10,8,256]{2,1,0:T(8,128)S(1)}, f32[10,8,256]{2,1,0:T(8,128)S(1)}, u32[]{:S(2)}, u32[]{:S(2)}) collective-permute-start(f32[10,8,256]{2,1,0:T(8,128)S(1)} %get-tuple-element.24), channel_id=1, source_target_pairs={{0,4},{4,8},{8,12},{12,16},{16,20},{20,24},{24,28},{1,5},{5,9},{9,... | collective-permute-start | bytes 245768 | tf_op jit(solution)/shard_map/ppermute | solution.py:268
  37.6 1.3 %collective-permute-start.5 = (f32[10,8,256]{2,1,0:T(8,128)S(1)}, f32[10,8,256]{2,1,0:T(8,128)S(1)}, u32[]{:S(2)}, u32[]{:S(2)}) collective-permute-start(f32[10,8,256]{2,1,0:T(8,128)S(1)} %get-tuple-element.25), channel_id=1, source_target_pairs={{4,0},{8,4},{12,8},{16,12},{20,16},{24,20},{28,24},{5,1},{9,5},{13... | collective-permute-start | bytes 245768 | tf_op jit(solution)/shard_map/ppermute | solution.py:268
  38.9 0.0 collective-permute-done.below.fixed_low
  38.9 0.0 collective-permute-done.1.above.fixed_high
  38.9 0.4 pack.2
  39.3 1.5 %collective-permute-start.2 = (f32[3,32,128]{2,1,0:T(8,128)S(1)}, f32[3,32,128]{2,1,0:T(8,128)S(1)}, u32[]{:S(2)}, u32[]{:S(2)}) collective-permute-start(f32[3,32,128]{2,1,0:T(8,128)S(1)} %get-tuple-element.20), channel_id=1, source_target_pairs={{0,1},{1,2},{2,3},{4,5},{5,6},{6,7},{8,9},{9,10},{10,11},{12,13},{... | collective-permute-start | bytes 147464 | tf_op jit(solution)/shard_map/ppermute | solution.py:268
  40.8 1.3 %collective-permute-start.3 = (f32[3,32,128]{2,1,0:T(8,128)S(1)}, f32[3,32,128]{2,1,0:T(8,128)S(1)}, u32[]{:S(2)}, u32[]{:S(2)}) collective-permute-start(f32[3,32,128]{2,1,0:T(8,128)S(1)} %get-tuple-element.21), channel_id=1, source_target_pairs={{1,0},{2,1},{3,2},{5,4},{6,5},{7,6},{9,8},{10,9},{11,10},{13,12},{... | collective-permute-start | bytes 147464 | tf_op jit(solution)/shard_map/ppermute | solution.py:268
  42.1 0.0 collective-permute-done.4
  42.1 1.8 %collective-permute-done.5 = f32[10,8,256]{2,1,0:T(8,128)S(1)} collective-permute-done((f32[10,8,256]{2,1,0:T(8,128)S(1)}, f32[10,8,256]{2,1,0:T(8,128)S(1)}, u32[]{:S(2)}, u32[]{:S(2)}) %collective-permute-start.5) | collective-permute-done | bytes 81952 | tf_op jit(solution)/shard_map/ppermute | solution.py:268
  43.9 0.2 pack.3
  44.1 2.3 %collective-permute-start.6 = (f32[1,32,128]{2,1,0:T(8,128)S(1)}, f32[1,32,128]{2,1,0:T(8,128)S(1)}, u32[]{:S(2)}, u32[]{:S(2)}) collective-permute-start(f32[1,32,128]{2,1,0:T(8,128)S(1)} %get-tuple-element.26), channel_id=1, source_target_pairs={{0,1},{1,2},{2,3},{4,5},{5,6},{6,7},{8,9},{9,10},{10,11},{12,13},{... | collective-permute-start | bytes 49160 | tf_op jit(solution)/shard_map/ppermute | solution.py:268
  46.4 1.3 %collective-permute-start.7 = (f32[1,32,128]{2,1,0:T(8,128)S(1)}, f32[1,32,128]{2,1,0:T(8,128)S(1)}, u32[]{:S(2)}, u32[]{:S(2)}) collective-permute-start(f32[1,32,128]{2,1,0:T(8,128)S(1)} %get-tuple-element.27), channel_id=1, source_target_pairs={{1,0},{2,1},{3,2},{5,4},{6,5},{7,6},{9,8},{10,9},{11,10},{13,12},{... | collective-permute-start | bytes 49160 | tf_op jit(solution)/shard_map/ppermute | solution.py:268
  47.7 0.0 collective-permute-done.2.fixed_left
  47.8 0.0 collective-permute-done.3.fixed_right
  47.8 0.0 collective-permute-done.6.src_left
  47.8 3.0 %collective-permute-done.7.src_right = f32[1,32,128]{2,1,0:T(8,128)S(1)} collective-permute-done((f32[1,32,128]{2,1,0:T(8,128)S(1)}, f32[1,32,128]{2,1,0:T(8,128)S(1)}, u32[]{:S(2)}, u32[]{:S(2)}) %collective-permute-start.7) | collective-permute-done | bytes 16416 | tf_op jit(solution)/shard_map/ppermute | solution.py:268
  50.8 15.4 %newton.1 = (f32[10,32,256]{2,1,0:T(8,128)}, f32[960,128]{1,0:T(8,128)S(1)}) custom-call(f32[3,10,32,256]{3,2,1,0:T(8,128)S(1)} %get-tuple-element.17.middle.fixed, f32[3,10,8,256]{3,2,1,0:T(8,128)S(1)} %collective-permute-done.below.fixed_low, f32[3,10,8,256]{3,2,1,0:T(8,128)S(1)} %collective-permute-done.1.above.fixed_high, ...), custom_call_target="tpu_custom_call" | custom-call | tf_op jit(solution)/shard_map/newton/pallas_call | solution.py:545
  66.2 20.9 %all_to_all.18 = f32[32,3840,1]{1,2,0:T(1,128)S(1)} all-to-all(f32[32,3840,1]{1,2,0:T(1,128)S(1)} %bitcast.16), channel_id=1, replica_groups=mesh['gx'=8,'gy'=4] {'gx','gy'}, dimensions={0} | all-to-all | bytes 983040 | tf_op jit(solution)/shard_map/all_to_all | solution.py:641
  87.1 2.2 %combine.1 = f32[10,8192]{1,0:T(8,128)} custom-call(s32[1,128]{1,0:T(1,128)S(1)} %get-tuple-element.30.starts, f32[960,128]{1,0:T(8,128)S(1)} %bitcast.13), custom_call_target="tpu_custom_call" | custom-call | tf_op jit(solution)/shard_map/combine/pallas_call | solution.py:591
Async XLA Ops:
  0.6 11.2 %copy-start.3 = (f32[10,32,256]{2,1,0:T(8,128)S(1)}, f32[10,32,256]{2,1,0:T(8,128)}, u32[]{:S(2)}) copy-start(f32[10,32,256]{2,1,0:T(8,128)} %pressure.1) | copy-start | bytes 983044
  4.4 7.4 %copy-start = (f32[10,32,256]{2,1,0:T(8,128)S(1)}, f32[10,32,256]{2,1,0:T(8,128)}, u32[]{:S(2)}) copy-start(f32[10,32,256]{2,1,0:T(8,128)} %conductivity.1) | copy-start | bytes 983044
  4.4 7.4 %copy-start.1 = (s32[10,32,256]{2,1,0:T(8,128)S(1)}, s32[10,32,256]{2,1,0:T(8,128)}, u32[]{:S(2)}) copy-start(s32[10,32,256]{2,1,0:T(8,128)} %freeze.1) | copy-start | bytes 983044
  4.5 7.4 %copy-start.2 = (f32[10,32,256]{2,1,0:T(8,128)S(1)}, f32[10,32,256]{2,1,0:T(8,128)}, u32[]{:S(2)}) copy-start(f32[10,32,256]{2,1,0:T(8,128)} %porosity.1) | copy-start | bytes 983044
  4.5 23.3 %all-to-all-start = ((f32[32,4224,1]{1,2,0:T(1,128)}), f32[32,4224,1]{1,2,0:T(1,128)S(1)}, u32[]{:S(2)}, u32[]{:S(2)}) async-start(f32[32,4224,1]{1,2,0:T(1,128)} %bitcast.4), calls=%async_computation | async-start | bytes 1081344 | tf_op jit(solution)/shard_map/all_to_all | solution.py:624
  11.8 15.9 %copy-start.4 = (s32[32,256]{1,0:T(8,128)S(1)}, s32[32,256]{1,0:T(8,128)}, u32[]{:S(2)}) copy-start(s32[32,256]{1,0:T(8,128)} %mask.1) | copy-start | bytes 98308
  12.0 26.9 %collective-permute-start = (f32[3,10,8,256]{3,2,1,0:T(8,128)S(1)}, f32[3,10,8,256]{3,2,1,0:T(8,128)S(1)}, u32[]{:S(2)}, u32[]{:S(2)}) collective-permute-start(f32[3,10,8,256]{3,2,1,0:T(8,128)S(1)} %get-tuple-element.18), channel_id=1, source_target_pairs={{0,4},{4,8},{8,12},{12,16},{16,20},{20,24},{24,28},{1,5},{5,9},{9,... | collective-permute-start | bytes 737288 | tf_op jit(solution)/shard_map/ppermute | solution.py:268
  15.7 23.2 %collective-permute-start.1 = (f32[3,10,8,256]{3,2,1,0:T(8,128)S(1)}, f32[3,10,8,256]{3,2,1,0:T(8,128)S(1)}, u32[]{:S(2)}, u32[]{:S(2)}) collective-permute-start(f32[3,10,8,256]{3,2,1,0:T(8,128)S(1)} %get-tuple-element.19), channel_id=1, source_target_pairs={{4,0},{8,4},{12,8},{16,12},{20,16},{24,20},{28,24},{5,1},{9,5},{13... | collective-permute-start | bytes 737288 | tf_op jit(solution)/shard_map/ppermute | solution.py:268
  34.3 7.8 %collective-permute-start.4 = (f32[10,8,256]{2,1,0:T(8,128)S(1)}, f32[10,8,256]{2,1,0:T(8,128)S(1)}, u32[]{:S(2)}, u32[]{:S(2)}) collective-permute-start(f32[10,8,256]{2,1,0:T(8,128)S(1)} %get-tuple-element.24), channel_id=1, source_target_pairs={{0,4},{4,8},{8,12},{12,16},{16,20},{20,24},{24,28},{1,5},{5,9},{9,... | collective-permute-start | bytes 245768 | tf_op jit(solution)/shard_map/ppermute | solution.py:268
  37.6 6.3 %collective-permute-start.5 = (f32[10,8,256]{2,1,0:T(8,128)S(1)}, f32[10,8,256]{2,1,0:T(8,128)S(1)}, u32[]{:S(2)}, u32[]{:S(2)}) collective-permute-start(f32[10,8,256]{2,1,0:T(8,128)S(1)} %get-tuple-element.25), channel_id=1, source_target_pairs={{4,0},{8,4},{12,8},{16,12},{20,16},{24,20},{28,24},{5,1},{9,5},{13... | collective-permute-start | bytes 245768 | tf_op jit(solution)/shard_map/ppermute | solution.py:268
  39.3 8.4 %collective-permute-start.2 = (f32[3,32,128]{2,1,0:T(8,128)S(1)}, f32[3,32,128]{2,1,0:T(8,128)S(1)}, u32[]{:S(2)}, u32[]{:S(2)}) collective-permute-start(f32[3,32,128]{2,1,0:T(8,128)S(1)} %get-tuple-element.20), channel_id=1, source_target_pairs={{0,1},{1,2},{2,3},{4,5},{5,6},{6,7},{8,9},{9,10},{10,11},{12,13},{... | collective-permute-start | bytes 147464 | tf_op jit(solution)/shard_map/ppermute | solution.py:268
  40.8 6.9 %collective-permute-start.3 = (f32[3,32,128]{2,1,0:T(8,128)S(1)}, f32[3,32,128]{2,1,0:T(8,128)S(1)}, u32[]{:S(2)}, u32[]{:S(2)}) collective-permute-start(f32[3,32,128]{2,1,0:T(8,128)S(1)} %get-tuple-element.21), channel_id=1, source_target_pairs={{1,0},{2,1},{3,2},{5,4},{6,5},{7,6},{9,8},{10,9},{11,10},{13,12},{... | collective-permute-start | bytes 147464 | tf_op jit(solution)/shard_map/ppermute | solution.py:268
  44.1 3.6 %collective-permute-start.6 = (f32[1,32,128]{2,1,0:T(8,128)S(1)}, f32[1,32,128]{2,1,0:T(8,128)S(1)}, u32[]{:S(2)}, u32[]{:S(2)}) collective-permute-start(f32[1,32,128]{2,1,0:T(8,128)S(1)} %get-tuple-element.26), channel_id=1, source_target_pairs={{0,1},{1,2},{2,3},{4,5},{5,6},{6,7},{8,9},{9,10},{10,11},{12,13},{... | collective-permute-start | bytes 49160 | tf_op jit(solution)/shard_map/ppermute | solution.py:268
  46.4 4.3 %collective-permute-start.7 = (f32[1,32,128]{2,1,0:T(8,128)S(1)}, f32[1,32,128]{2,1,0:T(8,128)S(1)}, u32[]{:S(2)}, u32[]{:S(2)}) collective-permute-start(f32[1,32,128]{2,1,0:T(8,128)S(1)} %get-tuple-element.27), channel_id=1, source_target_pairs={{1,0},{2,1},{3,2},{5,4},{6,5},{7,6},{9,8},{10,9},{11,10},{13,12},{... | collective-permute-start | bytes 49160 | tf_op jit(solution)/shard_map/ppermute | solution.py:268

commit v2 on v1

--- a/solution.py
+++ b/solution.py
@@ -14,8 +14,8 @@
 GROUPS = LANES // HALO
 
 
-def params():
-    return pltpu.CompilerParams(vmem_limit_bytes=48 * 2**20)
+def params(mebibytes=16):
+    return pltpu.CompilerParams(vmem_limit_bytes=mebibytes * 2**20)
 
 
 def saturation(field):
@@ -352,23 +352,26 @@
     )(conductivity, freeze, porosity, pressure)
 
 
-def gather_slots(order, incoming, table, reply, layers, cells_x, cells_y):
+def gather_slots(order, incoming, table, split, reply, layers, cells_x, cells_y, turned):
     fields = layers + 1
     chunks = incoming.shape[0] // fields
     sub = lax.broadcasted_iota(jnp.int32, (ROWS, LANES), 0)
+    row_x = lax.broadcasted_iota(jnp.int32, (cells_x, LANES), 0)
+    row_y = lax.broadcasted_iota(jnp.int32, (cells_y, LANES), 0)
     across = cells_y // LANES
     groups = cells_x // ROWS * across
-
-    def one(c):
-        cell = incoming[pl.ds(c * fields + layers, 1), :].astype(jnp.int32)
-        cell = jnp.broadcast_to(jnp.maximum(cell, 0), (ROWS, LANES))
+    half = split.shape[0] // 2
+    together = max(b for b in (8, 4, 3, 2, 1) if chunks % b == 0)
+
+    def looked_up(cell):
+        cell = jnp.broadcast_to(cell, (ROWS, LANES))
         x = cell // cells_y
         y = cell - x * cells_y
         lane = y % LANES
         group = (x // ROWS) * across + y // LANES
         wanted = x % ROWS == sub
         rows = []
-        for k in range(layers):
+        for k in range(turned):
             value = jnp.zeros((ROWS, LANES), jnp.float32)
             for g in range(groups):
                 first = HALO + g // across * ROWS
@@ -377,187 +380,291 @@
                 value = jnp.where(group == g, found, value)
             value = jnp.where(wanted, value, 0.0)
             rows.append(jnp.sum(value, axis=0, keepdims=True))
-        reply[pl.ds(c * layers, layers), :] = jnp.concatenate(rows, axis=0)
-
-    together = max(b for b in (4, 3, 2, 1) if chunks % b == 0)
+        return rows
 
     def body(i, carry):
-        for b in range(together):
-            one(order[i * together + b])
+        places = [order[i * together + b] for b in range(together)]
+        cells = []
+        onehots = []
+        for c in places:
+            cell = jnp.maximum(incoming[pl.ds(c * fields + layers, 1), :].astype(jnp.int32), 0)
+            cells.append(cell)
+            onehots.append((row_y == cell % cells_y).astype(jnp.float32).astype(jnp.bfloat16))
+        product = jnp.dot(
+            split[...], jnp.concatenate(onehots, axis=1), preferred_element_type=jnp.float32
+        )
+        for b, c in enumerate(places):
+            rows = looked_up(cells[b])
+            here = row_x == cells[b] // cells_y
+            span = slice(b * LANES, (b + 1) * LANES)
+            for k in range(layers - turned):
+                upper = product[k * cells_x : (k + 1) * cells_x, span]
+                lower = product[half + k * cells_x : half + (k + 1) * cells_x, span]
+                found = jnp.where(here, upper + lower, 0.0)
+                rows.append(jnp.sum(found, axis=0, keepdims=True))
+            reply[pl.ds(c * layers, layers), :] = jnp.concatenate(rows, axis=0)
         return carry
 
     lax.fori_loop(0, (order[chunks] + together - 1) // together, body, 0)
 
 
-def newton_kernel(layers, cells_x, cells_y):
-    high_x = cells_x + 2 * HALO
-    wide = cells_y + LANES
-
-    def up(v):
-        return pltpu.roll(v, high_x - 1, 0)
-
-    def down(v):
+class Stencil:
+    def __init__(self, layers, cells_x, cells_y):
+        self.layers, self.cells_x, self.cells_y = layers, cells_x, cells_y
+        self.high_x, self.wide = cells_x + 2 * HALO, cells_y + LANES
+
+    def up(self, v):
+        return pltpu.roll(v, self.high_x - 1, 0)
+
+    def down(self, v):
         return pltpu.roll(v, 1, 0)
 
-    def right(v):
-        return pltpu.roll(v, wide - 1, 1)
-
-    def left(v):
+    def right(self, v):
+        return pltpu.roll(v, self.wide - 1, 1)
+
+    def left(self, v):
         return pltpu.roll(v, 1, 1)
 
-    def each_layer(do):
-        for k in range(layers):
+    def each_layer(self, do):
+        for k in range(self.layers):
             do(k)
 
-    def kernel(
-        fixed, fixed_low, fixed_high, fixed_left, fixed_right,
-        src, src_low, src_high, src_left, src_right, incoming, order,
-        new_pressure, reply,
-        perm, poro, source, pres, stored,
-        tx, ty, tz, rel, gz, flow,
-        ax, bx, ay, by, az, bz, resid, update,
-    ):
+    def widen(self, dest, field, middle, low, high, side_left, side_right):
+        layers, cells_x, cells_y = self.layers, self.cells_x, self.cells_y
         lane = lax.broadcasted_iota(jnp.int32, (ROWS, LANES), 1)
-        last = cells_x // ROWS + 1
-
-        def widen(dest, field, middle, low, high, side_left, side_right):
-            dest[:, HALO : HALO + cells_x, :cells_y] = middle[field]
-            dest[:, :HALO, :cells_y] = low[field]
-            dest[:, HALO + cells_x :, :cells_y] = high[field]
-            for k, t, place, group in tile_places(layers, cells_x):
-                rows = slice(place * ROWS, (place + 1) * ROWS)
-                turn = (LANES - HALO - group * HALO) % LANES
-                a = side_left[field, rows, :]
-                a = pltpu.roll(a, turn, 1) if turn else a
-                turn = (-group * HALO) % LANES
-                b = side_right[field, rows, :]
-                b = pltpu.roll(b, turn, 1) if turn else b
-                tile = jnp.where(lane < HALO, b, jnp.where(lane >= LANES - HALO, a, 0.0))
-                dest[k, t * ROWS : (t + 1) * ROWS, cells_y:] = tile
-
-        widen(perm, 0, fixed, fixed_low, fixed_high, fixed_left, fixed_right)
-        widen(poro, 1, fixed, fixed_low, fixed_high, fixed_left, fixed_right)
-        widen(pres, 2, fixed, fixed_low, fixed_high, fixed_left, fixed_right)
-        widen(source, 0, src, src_low, src_high, src_left, src_right)
-
+        dest[:, HALO : HALO + cells_x, :cells_y] = middle[field]
+        dest[:, :HALO, :cells_y] = low[field]
+        dest[:, HALO + cells_x :, :cells_y] = high[field]
+        for k, t, place, group in tile_places(layers, cells_x):
+            rows = slice(place * ROWS, (place + 1) * ROWS)
+            turn = (LANES - HALO - group * HALO) % LANES
+            a = side_left[field, rows, :]
+            a = pltpu.roll(a, turn, 1) if turn else a
+            turn = (-group * HALO) % LANES
+            b = side_right[field, rows, :]
+            b = pltpu.roll(b, turn, 1) if turn else b
+            tile = jnp.where(lane < HALO, b, jnp.where(lane >= LANES - HALO, a, 0.0))
+            dest[k, t * ROWS : (t + 1) * ROWS, cells_y:] = tile
+
+    def faces(self, perm, tx, ty, tz):
         def face(a, b):
             joined = a + b
             return a * b / jnp.where(joined > 0.0, joined, 1.0)
 
         def still(k):
             a = perm[k]
-            tx[k] = face(a, up(a))
-            ty[k] = face(a, right(a))
-            tz[k] = face(a, perm[min(k + 1, layers - 1)])
+            tx[k] = face(a, self.up(a))
+            ty[k] = face(a, self.right(a))
+            tz[k] = face(a, perm[min(k + 1, self.layers - 1)])
+
+        self.each_layer(still)
+
+    def linearize(self, pres, poro, stored, last_perm, tx, ty, tz, rel, gz, flow, weights, finish):
+        ax, bx, ay, by, az, bz = weights
+        layers = self.layers
+
+        def relative(k):
+            s = saturation(pres[k])
+            rel[k] = s * s * s
+
+        self.each_layer(relative)
+        nothing = jnp.zeros((self.high_x, self.wide), jnp.float32)
+        gz[0] = nothing
+        flow[0] = nothing
+
+        def vertical(k):
+            r = rel[k]
+            if k < layers - 1:
+                g = tz[k] * (r + rel[k + 1])
+                gz[k + 1] = g
+                flow[k + 1] = g * (pres[k] - pres[k + 1] + 1.0)
+            else:
+                gz[k + 1] = nothing
+                flow[k + 1] = last_perm * r
+
+        self.each_layer(vertical)
+
+        def linear(k):
+            p = pres[k]
+            r = rel[k]
+            gx = tx[k] * (r + self.up(r))
+            gy = ty[k] * (r + self.right(r))
+            fx = gx * (p - self.up(p))
+            fy = gy * (p - self.right(p))
+            gxd = self.down(gx)
+            gyd = self.left(gy)
+            s = saturation(p)
+            porous = poro[k]
+            residual = porous * (s - stored[k])
+            residual = residual + (fx - self.down(fx)) + (fy - self.left(fy))
+            residual = residual + (flow[k + 1] - flow[k])
+            gzd = gz[k]
+            gzu = gz[k + 1]
+            diagonal = porous * (jnp.maximum(-p, 0.0) * r)
+            diagonal = diagonal + (gx + gxd) + (gy + gyd) + (gzu + gzd)
+            diagonal = jnp.where(diagonal > 0.0, diagonal, 1.0)
+            scale = OMEGA / diagonal
+            ax[k] = scale * gx
+            bx[k] = scale * gxd
+            ay[k] = scale * gy
+            by[k] = scale * gyd
+            az[k] = scale * gzu
+            bz[k] = scale * gzd
+            finish(k, residual, scale)
+
+        self.each_layer(linear)
+
+    def sweeps(self, pres, weights, resid, update):
+        ax, bx, ay, by, az, bz = weights
+        layers = self.layers
+        for sweep in range(SWEEPS - 1):
+            old = sweep % 2
+            new = 1 - old
+
+            def smooth(k):
+                u = update[old, k]
+                v = (1.0 - OMEGA) * u - resid[k]
+                v = v + ax[k] * self.up(u) + bx[k] * self.down(u)
+                v = v + ay[k] * self.right(u) + by[k] * self.left(u)
+                v = v + az[k] * update[old, min(k + 1, layers - 1)]
+                v = v + bz[k] * update[old, max(k - 1, 0)]
+                update[new, k] = v
+                if sweep == SWEEPS - 2:
+                    pres[k] = pres[k] + v
+
+            self.each_layer(smooth)
+
+
+def begin_kernel(grid):
+    def kernel(
+        fixed, low, high, side_left, side_right,
+        pres, poro, stored, last_perm, tx, ty, tz, ax, bx, ay, by, az, bz, resid, scales,
+        perm, rel, gz, flow,
+    ):
+        sides = (low, high, side_left, side_right)
+        grid.widen(perm, 0, fixed, *sides)
+        grid.widen(poro, 1, fixed, *sides)
+        grid.widen(pres, 2, fixed, *sides)
+        grid.faces(perm, tx, ty, tz)
+        last_perm[...] = perm[grid.layers - 1]
+
+        def keep(k):
             stored[k] = saturation(pres[k])
 
-        each_layer(still)
-
-        for newton_step in range(NEWTON):
-
-            def relative(k):
-                s = saturation(pres[k])
-                rel[k] = s * s * s
-
-            each_layer(relative)
-
-            def vertical(k):
-                r = rel[k]
-                below = min(k + 1, layers - 1)
-                g = tz[k] * (r + rel[below])
-                if k < layers - 1:
-                    gz[k + 1] = g
-                    flow[k + 1] = g * (pres[k] - pres[below] + 1.0)
-                else:
-                    gz[k + 1] = jnp.zeros_like(g)
-                    flow[k + 1] = perm[k] * r
-
-            gz[0] = jnp.zeros((high_x, wide), jnp.float32)
-            flow[0] = jnp.zeros((high_x, wide), jnp.float32)
-            each_layer(vertical)
-
-            def linear(k):
-                p = pres[k]
-                r = rel[k]
-                gx = tx[k] * (r + up(r))
-                gy = ty[k] * (r + right(r))
-                fx = gx * (p - up(p))
-                fy = gy * (p - right(p))
-                gxd = down(gx)
-                gyd = left(gy)
-                s = saturation(p)
-                porous = poro[k]
-                residual = porous * (s - stored[k])
-                residual = residual + (fx - down(fx)) + (fy - left(fy))
-                residual = residual + (flow[k + 1] - flow[k]) - source[k]
-                gzd = gz[k]
-                gzu = gz[k + 1]
-                diagonal = porous * (jnp.maximum(-p, 0.0) * r)
-                diagonal = diagonal + (gx + gxd) + (gy + gyd) + (gzu + gzd)
-                diagonal = jnp.where(diagonal > 0.0, diagonal, 1.0)
-                scale = OMEGA / diagonal
-                ax[k] = scale * gx
-                bx[k] = scale * gxd
-                ay[k] = scale * gy
-                by[k] = scale * gyd
-                az[k] = scale * gzu
-                bz[k] = scale * gzd
-                residual = scale * residual
+        grid.each_layer(keep)
+
+        def finish(k, residual, scale):
+            resid[k] = scale * residual
+            scales[k] = scale
+
+        grid.linearize(
+            pres, poro, stored, last_perm[...], tx, ty, tz, rel, gz, flow,
+            (ax, bx, ay, by, az, bz), finish,
+        )
+
+    return kernel
+
+
+def begin(fixed, layers, cells_x, cells_y):
+    grid = Stencil(layers, cells_x, cells_y)
+    shape = (layers, grid.high_x, grid.wide)
+    field = jax.ShapeDtypeStruct(shape, jnp.float32)
+    plane = jax.ShapeDtypeStruct(shape[1:], jnp.float32)
+    vmem = pl.BlockSpec(memory_space=pltpu.VMEM)
+    outs = (field,) * 3 + (plane,) + (field,) * 11
+    cells = layers * grid.high_x * grid.wide
+    return pl.pallas_call(
+        begin_kernel(grid),
+        out_shape=outs,
+        in_specs=[vmem] * 5,
+        out_specs=(vmem,) * len(outs),
+        scratch_shapes=[pltpu.VMEM(shape, jnp.float32)] * 2
+        + [pltpu.VMEM((layers + 1,) + shape[1:], jnp.float32)] * 2,
+        compiler_params=params(24),
+        cost_estimate=pl.CostEstimate(
+            flops=100 * cells, transcendentals=4 * cells, bytes_accessed=0
+        ),
+        name="begin",
+    )(*fixed)
+
+
+def newton_kernel(grid, turned):
+    layers, cells_x, cells_y = grid.layers, grid.cells_x, grid.cells_y
+
+    def kernel(
+        pres0, poro, stored, last_perm, tx, ty, tz,
+        ax0, bx0, ay0, by0, az0, bz0, resid0, scales,
+        src, src_low, src_high, src_left, src_right, incoming, order,
+        new_pressure, reply,
+        source, pres, rel, gz, flow, ax, bx, ay, by, az, bz, resid, update, split,
+    ):
+        grid.widen(source, 0, src, src_low, src_high, src_left, src_right)
+
+        def first(k):
+            pres[k] = pres0[k]
+            residual = resid0[k] - scales[k] * source[k]
+            resid[k] = residual
+            update[0, k] = -residual
+
+        grid.each_layer(first)
+        grid.sweeps(pres, (ax0, bx0, ay0, by0, az0, bz0), resid, update)
+        weights = (ax, bx, ay, by, az, bz)
+        for newton_step in range(1, NEWTON):
+
+            def finish(k, residual, scale):
+                residual = scale * (residual - source[k])
                 resid[k] = residual
                 update[0, k] = -residual
 
-            each_layer(linear)
-
-            for sweep in range(SWEEPS - 1):
-                old = sweep % 2
-                new = 1 - old
-
-                def smooth(k):
-                    u = update[old, k]
-                    v = (1.0 - OMEGA) * u - resid[k]
-                    v = v + ax[k] * up(u) + bx[k] * down(u)
-                    v = v + ay[k] * right(u) + by[k] * left(u)
-                    v = v + az[k] * update[old, min(k + 1, layers - 1)]
-                    v = v + bz[k] * update[old, max(k - 1, 0)]
-                    update[new, k] = v
-                    if sweep == SWEEPS - 2:
-                        pres[k] = pres[k] + v
-
-                each_layer(smooth)
-
-        def finish(k):
+            grid.linearize(
+                pres, poro, stored, last_perm[...], tx, ty, tz, rel, gz, flow, weights, finish
+            )
+            grid.sweeps(pres, weights, resid, update)
+
+        half = split.shape[0] // 2
+        for k in range(layers):
             p = pres[k, HALO : HALO + cells_x, :cells_y]
             new_pressure[k] = p
-            rel[k, HALO : HALO + cells_x, :cells_y] = saturation(p)
-
-        each_layer(finish)
-        gather_slots(order, incoming, rel, reply, layers, cells_x, cells_y)
+            s = saturation(p)
+            if k < turned:
+                rel[k, HALO : HALO + cells_x, :cells_y] = s
+            else:
+                row = (k - turned) * cells_x
+                upper = s.astype(jnp.bfloat16)
+                split[row : row + cells_x, :] = upper
+                lower = (s - upper.astype(jnp.float32)).astype(jnp.bfloat16)
+                split[half + row : half + row + cells_x, :] = lower
+        gather_slots(order, incoming, rel, split, reply, layers, cells_x, cells_y, turned)
 
     return kernel
 
 
-def newton(fixed, source, incoming, order, layers, cells_x, cells_y):
+def newton(begun, source, incoming, order, layers, cells_x, cells_y):
+    grid = Stencil(layers, cells_x, cells_y)
+    turned = 5
     chunks = incoming.shape[0] // (layers + 1)
-    high_x, wide = cells_x + 2 * HALO, cells_y + LANES
-    field = pltpu.VMEM((layers, high_x, wide), jnp.float32)
-    taller = pltpu.VMEM((layers + 1, high_x, wide), jnp.float32)
+    shape = (layers, grid.high_x, grid.wide)
+    field = pltpu.VMEM(shape, jnp.float32)
+    taller = pltpu.VMEM((layers + 1,) + shape[1:], jnp.float32)
     vmem = pl.BlockSpec(memory_space=pltpu.VMEM)
     return pl.pallas_call(
-        newton_kernel(layers, cells_x, cells_y),
+        newton_kernel(grid, turned),
         out_shape=(
             jax.ShapeDtypeStruct((layers, cells_x, cells_y), jnp.float32),
             jax.ShapeDtypeStruct((chunks * layers, LANES), jnp.float32),
         ),
-        in_specs=[vmem] * 11 + [pl.BlockSpec(memory_space=pltpu.SMEM)],
+        in_specs=[vmem] * 21 + [pl.BlockSpec(memory_space=pltpu.SMEM)],
         out_specs=(vmem, vmem),
-        scratch_shapes=[field] * 5
-        + [field] * 4
+        scratch_shapes=[field] * 3
         + [taller] * 2
         + [field] * 7
-        + [pltpu.VMEM((2, layers, high_x, wide), jnp.float32)],
-        compiler_params=params(),
+        + [
+            pltpu.VMEM((2,) + shape, jnp.float32),
+            pltpu.VMEM((2 * (layers - turned) * cells_x, cells_y), jnp.bfloat16),
+        ],
+        compiler_params=params(32),
         name="newton",
-    )(*fixed, *source, incoming, order)
+    )(*begun, *source, incoming, order)
 
 
 def combine_kernel(layers, devices, capacity):
@@ -622,22 +729,23 @@
         clm_block, clm_cell, precip, evap_demand, root_share, sat_before, devices, capacity
     )
     flat = lax.all_to_all(outgoing.reshape(-1), axes, split_axis=0, concat_axis=0, tiled=True)
-    incoming = flat.reshape(outgoing.shape)
 
     fixed, low, high = prepare(conductivity, freeze_state, porosity, pressure)
     below, above = both_ways(low, high, "gx")
     to_left, to_right = pack(fixed, below, above)
     side_left, side_right = both_ways(to_left, to_right, "gy")
     fixed = (fixed, below, above, side_left, side_right)
+    incoming = flat.reshape(outgoing.shape)
 
     source, low, high, order = scatter(incoming, land_mask, layers, cells_x, cells_y)
     below, above = both_ways(low, high, "gx")
+    begun = begin(fixed, layers, cells_x, cells_y)
     source, below, above = source[None], below[None], above[None]
     to_left, to_right = pack(source, below, above)
     side_left, side_right = both_ways(to_left, to_right, "gy")
     source = (source, below, above, side_left, side_right)
 
-    new_pressure, reply = newton(fixed, source, incoming, order, layers, cells_x, cells_y)
+    new_pressure, reply = newton(begun, source, incoming, order, layers, cells_x, cells_y)
     flat = lax.all_to_all(reply.reshape(-1), axes, split_axis=0, concat_axis=0, tiled=True)
     returned = combine(starts, flat.reshape(reply.shape), layers, columns, devices, capacity)
     return (new_pressure, returned)

time: 89.8 us -> 86.4 us (0.962)
  waiting for transfers between devices: 15.5 us -> 12.8 us
  Pallas kernels: 28.7 us -> 27 us
  blocking collectives: 20.9 us -> 22.1 us
    ppermute x4, waiting for transfers between devices: 4.79 us -> 2.01 us  [both_ways(): lax.ppermute(low_end, axis, backward)]
    pallas_call x1 -> x2, Pallas kernels: 15.4 us -> 13.7 us  [the longest x1 10.9 us: newton(): pl.pallas_call(newton_kernel(grid, turned), out_shape=(jax.ShapeDtypeStru...]
    all_to_all x1, blocking collectives: 20.9 us -> 22.1 us  [on_device(): lax.all_to_all(reply.reshape(-1), axes, split_axis=0, concat_axis=0, tile...]
  transfers between devices with their start and end apart: 9 -> 9, of which waited for: 3 -> 3; matrix products, arithmetic and copies ran while one was open for 0% -> 0% of each run, Pallas kernels for 8% -> 12%
where the time goes in v2:
time: 86.4 us; the launch traced here: 86 us
  Pallas kernels  27 us (31%)
  starting transfers between devices  23.2 us (27%)
  blocking collectives  22.1 us (26%)
  waiting for transfers between devices  12.8 us (15%)
  between operations  0.87 us (1%)
    all_to_all x1, blocking collectives, on_device(): lax.all_to_all(reply.reshape(-1), axes, split_axis=0, concat_axis=0, tile...  22.1 us
    pallas_call x1, Pallas kernels, newton(): pl.pallas_call(newton_kernel(grid, turned), out_shape=(jax.ShapeDtypeStru...  10.9 us
    all_to_all x1, waiting for transfers between devices, on_device(): lax.all_to_all(outgoing.reshape(-1), axes, split_axis=0, concat_axis=0, t...  10.7 us
    ppermute x4, starting transfers between devices, both_ways(): lax.ppermute(high_end, axis, forward)  10.7 us
    all_to_all x1, starting transfers between devices, on_device(): lax.all_to_all(outgoing.reshape(-1), axes, split_axis=0, concat_axis=0, t...  7.33 us
    pallas_call x1, Pallas kernels, scatter(): pl.pallas_call(scatter_kernel(layers, cells_x, cells_y, batch), out_shape...  6.59 us
    ppermute x4, starting transfers between devices, both_ways(): lax.ppermute(low_end, axis, backward)  5.17 us
    pallas_call x1, Pallas kernels, dispatch(): pl.pallas_call(dispatch_kernel(layers, devices, capacity), out_shape=(jax...  3.79 us
  transfers between devices with their start and end apart: 9, of which 3 were waited for; matrix products, arithmetic and copies ran while one was open for 0% of the time, Pallas kernels for 12%

profile of v2, /device:TPU:0, one launch (start us, length us, event | category | flops | bytes accessed | tf_op | source)
XLA Modules:
  0.0 86.0 jit_solution(11206320181107899752)
XLA Ops:
  0.6 0.0 copy-start.3
  0.6 3.8 %dispatch.1 = (f32[1056,128]{1,0:T(8,128)}, s32[1,128]{1,0:T(1,128)S(1)}) custom-call(s32[64,128]{1,0:T(8,128)} %bitcast.21, s32[64,128]{1,0:T(8,128)} %bitcast.22, f32[64,128]{1,0:T(8,128)} %bitcast.23, f32[64,128]{1,0:T(8,128)} %bitcast.24, f32[10,8192]{1,0:T(8,128)} %root_hbm.1, f32[10,8192]{1,0:T(8,128)} %sat_hbm.1), custom_call_target="tpu_custom_call" | custom-call | tf_op jit(solution)/shard_map/dispatch/pallas_call | solution.py:138
  4.4 0.0 copy-start
  4.5 0.0 copy-start.1
  4.5 0.0 copy-start.2
  4.5 7.3 %all-to-all-start = ((f32[32,4224,1]{1,2,0:T(1,128)}), f32[32,4224,1]{1,2,0:T(1,128)S(1)}, u32[]{:S(2)}, u32[]{:S(2)}) async-start(f32[32,4224,1]{1,2,0:T(1,128)} %bitcast.4), calls=%async_computation | async-start | bytes 1081344 | tf_op jit(solution)/shard_map/all_to_all | solution.py:731
  11.8 0.0 copy-done.3
  11.8 0.0 copy-done
  11.8 0.0 copy-done.1
  11.8 0.0 copy-done.2
  11.9 0.0 copy-start.4
  11.9 0.1 prepare.1
  12.0 3.7 %collective-permute-start = (f32[3,10,8,256]{3,2,1,0:T(8,128)S(1)}, f32[3,10,8,256]{3,2,1,0:T(8,128)S(1)}, u32[]{:S(2)}, u32[]{:S(2)}) collective-permute-start(f32[3,10,8,256]{3,2,1,0:T(8,128)S(1)} %get-tuple-element.33), channel_id=1, source_target_pairs={{0,4},{4,8},{8,12},{12,16},{16,20},{20,24},{24,28},{1,5},{5,9},{9,... | collective-permute-start | bytes 737288 | tf_op jit(solution)/shard_map/ppermute | solution.py:268
  15.7 1.3 %collective-permute-start.1 = (f32[3,10,8,256]{3,2,1,0:T(8,128)S(1)}, f32[3,10,8,256]{3,2,1,0:T(8,128)S(1)}, u32[]{:S(2)}, u32[]{:S(2)}) collective-permute-start(f32[3,10,8,256]{3,2,1,0:T(8,128)S(1)} %get-tuple-element.34), channel_id=1, source_target_pairs={{4,0},{8,4},{12,8},{16,12},{20,16},{24,20},{28,24},{5,1},{9,5},{13... | collective-permute-start | bytes 737288 | tf_op jit(solution)/shard_map/ppermute | solution.py:268
  17.0 10.7 %all-to-all-done = f32[32,4224,1]{1,2,0:T(1,128)S(1)} async-done(((f32[32,4224,1]{1,2,0:T(1,128)}), f32[32,4224,1]{1,2,0:T(1,128)S(1)}, u32[]{:S(2)}, u32[]{:S(2)}) %all-to-all-start) | async-done | bytes 540704 | tf_op jit(solution)/shard_map/all_to_all | solution.py:731
  27.7 0.0 copy-done.4
  27.7 6.6 %scatter.1 = (f32[10,32,256]{2,1,0:T(8,128)S(1)}, f32[10,8,256]{2,1,0:T(8,128)S(1)}, f32[10,8,256]{2,1,0:T(8,128)S(1)}, s32[97]{0:T(128)S(1)}) custom-call(f32[1056,128]{1,0:T(8,128)S(1)} %bitcast.11, s32[32,256]{1,0:T(8,128)S(1)} %copy-done.4), custom_call_target="tpu_custom_call" | custom-call | tf_op jit(solution)/shard_map/scatter/pallas_call | solution.py:243
  34.3 3.3 %collective-permute-start.4 = (f32[10,8,256]{2,1,0:T(8,128)S(1)}, f32[10,8,256]{2,1,0:T(8,128)S(1)}, u32[]{:S(2)}, u32[]{:S(2)}) collective-permute-start(f32[10,8,256]{2,1,0:T(8,128)S(1)} %get-tuple-element.54), channel_id=1, source_target_pairs={{0,4},{4,8},{8,12},{12,16},{16,20},{20,24},{24,28},{1,5},{5,9},{9,... | collective-permute-start | bytes 245768 | tf_op jit(solution)/shard_map/ppermute | solution.py:268
  37.6 1.3 %collective-permute-start.5 = (f32[10,8,256]{2,1,0:T(8,128)S(1)}, f32[10,8,256]{2,1,0:T(8,128)S(1)}, u32[]{:S(2)}, u32[]{:S(2)}) collective-permute-start(f32[10,8,256]{2,1,0:T(8,128)S(1)} %get-tuple-element.55), channel_id=1, source_target_pairs={{4,0},{8,4},{12,8},{16,12},{20,16},{24,20},{28,24},{5,1},{9,5},{13... | collective-permute-start | bytes 245768 | tf_op jit(solution)/shard_map/ppermute | solution.py:268
  38.9 0.0 collective-permute-done.below.low
  38.9 0.0 collective-permute-done.1.above.high
  38.9 0.4 pack.2
  39.3 1.5 %collective-permute-start.2 = (f32[3,32,128]{2,1,0:T(8,128)S(1)}, f32[3,32,128]{2,1,0:T(8,128)S(1)}, u32[]{:S(2)}, u32[]{:S(2)}) collective-permute-start(f32[3,32,128]{2,1,0:T(8,128)S(1)} %get-tuple-element.35), channel_id=1, source_target_pairs={{0,1},{1,2},{2,3},{4,5},{5,6},{6,7},{8,9},{9,10},{10,11},{12,13},{... | collective-permute-start | bytes 147464 | tf_op jit(solution)/shard_map/ppermute | solution.py:268
  40.8 1.3 %collective-permute-start.3 = (f32[3,32,128]{2,1,0:T(8,128)S(1)}, f32[3,32,128]{2,1,0:T(8,128)S(1)}, u32[]{:S(2)}, u32[]{:S(2)}) collective-permute-start(f32[3,32,128]{2,1,0:T(8,128)S(1)} %get-tuple-element.36), channel_id=1, source_target_pairs={{1,0},{2,1},{3,2},{5,4},{6,5},{7,6},{9,8},{10,9},{11,10},{13,12},{... | collective-permute-start | bytes 147464 | tf_op jit(solution)/shard_map/ppermute | solution.py:268
  42.1 0.0 collective-permute-done.4
  42.1 1.8 %collective-permute-done.5 = f32[10,8,256]{2,1,0:T(8,128)S(1)} collective-permute-done((f32[10,8,256]{2,1,0:T(8,128)S(1)}, f32[10,8,256]{2,1,0:T(8,128)S(1)}, u32[]{:S(2)}, u32[]{:S(2)}) %collective-permute-start.5) | collective-permute-done | bytes 81952 | tf_op jit(solution)/shard_map/ppermute | solution.py:268
  43.9 0.2 pack.3
  44.1 2.3 %collective-permute-start.6 = (f32[1,32,128]{2,1,0:T(8,128)S(1)}, f32[1,32,128]{2,1,0:T(8,128)S(1)}, u32[]{:S(2)}, u32[]{:S(2)}) collective-permute-start(f32[1,32,128]{2,1,0:T(8,128)S(1)} %get-tuple-element.56), channel_id=1, source_target_pairs={{0,1},{1,2},{2,3},{4,5},{5,6},{6,7},{8,9},{9,10},{10,11},{12,13},{... | collective-permute-start | bytes 49160 | tf_op jit(solution)/shard_map/ppermute | solution.py:268
  46.5 1.3 %collective-permute-start.7 = (f32[1,32,128]{2,1,0:T(8,128)S(1)}, f32[1,32,128]{2,1,0:T(8,128)S(1)}, u32[]{:S(2)}, u32[]{:S(2)}) collective-permute-start(f32[1,32,128]{2,1,0:T(8,128)S(1)} %get-tuple-element.57), channel_id=1, source_target_pairs={{1,0},{2,1},{3,2},{5,4},{6,5},{7,6},{9,8},{10,9},{11,10},{13,12},{... | collective-permute-start | bytes 49160 | tf_op jit(solution)/shard_map/ppermute | solution.py:268
  47.8 0.0 collective-permute-done.2.side_left
  47.8 0.0 collective-permute-done.3.side_right
  47.8 2.8 %begin.1 = (f32[10,48,384]{2,1,0:T(8,128)S(1)}, f32[10,48,384]{2,1,0:T(8,128)S(1)}, f32[10,48,384]{2,1,0:T(8,128)S(1)}, f32[48,384]{1,0:T(8,128)S(1)}, f32[10,48...) custom-call(f32[3,10,32,256]{3,2,1,0:T(8,128)S(1)} %get-tuple-elemen, ...), custom_call_target="tpu_custom_call" | custom-call | flops 18432000 | tf_op jit(solution)/shard_map/begin/pallas_call | solution.py:576
  50.6 0.0 collective-permute-done.6.src_left
  50.6 0.2 collective-permute-done.7.src_right
  50.8 10.9 %newton.1 = (f32[10,32,256]{2,1,0:T(8,128)}, f32[960,128]{1,0:T(8,128)S(1)}) custom-call(f32[10,48,384]{2,1,0:T(8,128)S(1)} %get-tuple-element.37.pres0, f32[10,48,384]{2,1,0:T(8,128)S(1)} %get-tuple-element.38.poro, f32[10,48,384]{2,1,0:T(8,128)S(1)} %get-tuple-element.39.stored, f32[48,384]{1,0:T(8,128)S(1)} %get-tuple-element.40.last_perm, ...), custom_call_target="tpu_custom_call" | custom-call | tf_op jit(solution)/shard_map/newton/pallas_call | solution.py:650
  61.7 22.1 %all_to_all.18 = f32[32,3840,1]{1,2,0:T(1,128)S(1)} all-to-all(f32[32,3840,1]{1,2,0:T(1,128)S(1)} %bitcast.16), channel_id=1, replica_groups=mesh['gx'=8,'gy'=4] {'gx','gy'}, dimensions={0} | all-to-all | bytes 983040 | tf_op jit(solution)/shard_map/all_to_all | solution.py:749
  83.8 2.2 %combine.1 = f32[10,8192]{1,0:T(8,128)} custom-call(s32[1,128]{1,0:T(1,128)S(1)} %get-tuple-element.60.starts, f32[960,128]{1,0:T(8,128)S(1)} %bitcast.13), custom_call_target="tpu_custom_call" | custom-call | tf_op jit(solution)/shard_map/combine/pallas_call | solution.py:698
Async XLA Ops:
  0.6 11.2 %copy-start.3 = (f32[10,32,256]{2,1,0:T(8,128)S(1)}, f32[10,32,256]{2,1,0:T(8,128)}, u32[]{:S(2)}) copy-start(f32[10,32,256]{2,1,0:T(8,128)} %pressure.1) | copy-start | bytes 983044
  4.4 7.4 %copy-start = (f32[10,32,256]{2,1,0:T(8,128)S(1)}, f32[10,32,256]{2,1,0:T(8,128)}, u32[]{:S(2)}) copy-start(f32[10,32,256]{2,1,0:T(8,128)} %conductivity.1) | copy-start | bytes 983044
  4.5 7.4 %copy-start.1 = (s32[10,32,256]{2,1,0:T(8,128)S(1)}, s32[10,32,256]{2,1,0:T(8,128)}, u32[]{:S(2)}) copy-start(s32[10,32,256]{2,1,0:T(8,128)} %freeze.1) | copy-start | bytes 983044
  4.5 7.4 %copy-start.2 = (f32[10,32,256]{2,1,0:T(8,128)S(1)}, f32[10,32,256]{2,1,0:T(8,128)}, u32[]{:S(2)}) copy-start(f32[10,32,256]{2,1,0:T(8,128)} %porosity.1) | copy-start | bytes 983044
  4.5 23.3 %all-to-all-start = ((f32[32,4224,1]{1,2,0:T(1,128)}), f32[32,4224,1]{1,2,0:T(1,128)S(1)}, u32[]{:S(2)}, u32[]{:S(2)}) async-start(f32[32,4224,1]{1,2,0:T(1,128)} %bitcast.4), calls=%async_computation | async-start | bytes 1081344 | tf_op jit(solution)/shard_map/all_to_all | solution.py:731
  11.9 15.9 %copy-start.4 = (s32[32,256]{1,0:T(8,128)S(1)}, s32[32,256]{1,0:T(8,128)}, u32[]{:S(2)}) copy-start(s32[32,256]{1,0:T(8,128)} %mask.1) | copy-start | bytes 98308
  12.0 26.9 %collective-permute-start = (f32[3,10,8,256]{3,2,1,0:T(8,128)S(1)}, f32[3,10,8,256]{3,2,1,0:T(8,128)S(1)}, u32[]{:S(2)}, u32[]{:S(2)}) collective-permute-start(f32[3,10,8,256]{3,2,1,0:T(8,128)S(1)} %get-tuple-element.33), channel_id=1, source_target_pairs={{0,4},{4,8},{8,12},{12,16},{16,20},{20,24},{24,28},{1,5},{5,9},{9,... | collective-permute-start | bytes 737288 | tf_op jit(solution)/shard_map/ppermute | solution.py:268
  15.7 23.2 %collective-permute-start.1 = (f32[3,10,8,256]{3,2,1,0:T(8,128)S(1)}, f32[3,10,8,256]{3,2,1,0:T(8,128)S(1)}, u32[]{:S(2)}, u32[]{:S(2)}) collective-permute-start(f32[3,10,8,256]{3,2,1,0:T(8,128)S(1)} %get-tuple-element.34), channel_id=1, source_target_pairs={{4,0},{8,4},{12,8},{16,12},{20,16},{24,20},{28,24},{5,1},{9,5},{13... | collective-permute-start | bytes 737288 | tf_op jit(solution)/shard_map/ppermute | solution.py:268
  34.3 7.8 %collective-permute-start.4 = (f32[10,8,256]{2,1,0:T(8,128)S(1)}, f32[10,8,256]{2,1,0:T(8,128)S(1)}, u32[]{:S(2)}, u32[]{:S(2)}) collective-permute-start(f32[10,8,256]{2,1,0:T(8,128)S(1)} %get-tuple-element.54), channel_id=1, source_target_pairs={{0,4},{4,8},{8,12},{12,16},{16,20},{20,24},{24,28},{1,5},{5,9},{9,... | collective-permute-start | bytes 245768 | tf_op jit(solution)/shard_map/ppermute | solution.py:268
  37.6 6.3 %collective-permute-start.5 = (f32[10,8,256]{2,1,0:T(8,128)S(1)}, f32[10,8,256]{2,1,0:T(8,128)S(1)}, u32[]{:S(2)}, u32[]{:S(2)}) collective-permute-start(f32[10,8,256]{2,1,0:T(8,128)S(1)} %get-tuple-element.55), channel_id=1, source_target_pairs={{4,0},{8,4},{12,8},{16,12},{20,16},{24,20},{28,24},{5,1},{9,5},{13... | collective-permute-start | bytes 245768 | tf_op jit(solution)/shard_map/ppermute | solution.py:268
  39.3 8.4 %collective-permute-start.2 = (f32[3,32,128]{2,1,0:T(8,128)S(1)}, f32[3,32,128]{2,1,0:T(8,128)S(1)}, u32[]{:S(2)}, u32[]{:S(2)}) collective-permute-start(f32[3,32,128]{2,1,0:T(8,128)S(1)} %get-tuple-element.35), channel_id=1, source_target_pairs={{0,1},{1,2},{2,3},{4,5},{5,6},{6,7},{8,9},{9,10},{10,11},{12,13},{... | collective-permute-start | bytes 147464 | tf_op jit(solution)/shard_map/ppermute | solution.py:268
  40.8 6.9 %collective-permute-start.3 = (f32[3,32,128]{2,1,0:T(8,128)S(1)}, f32[3,32,128]{2,1,0:T(8,128)S(1)}, u32[]{:S(2)}, u32[]{:S(2)}) collective-permute-start(f32[3,32,128]{2,1,0:T(8,128)S(1)} %get-tuple-element.36), channel_id=1, source_target_pairs={{1,0},{2,1},{3,2},{5,4},{6,5},{7,6},{9,8},{10,9},{11,10},{13,12},{... | collective-permute-start | bytes 147464 | tf_op jit(solution)/shard_map/ppermute | solution.py:268
  44.1 6.4 %collective-permute-start.6 = (f32[1,32,128]{2,1,0:T(8,128)S(1)}, f32[1,32,128]{2,1,0:T(8,128)S(1)}, u32[]{:S(2)}, u32[]{:S(2)}) collective-permute-start(f32[1,32,128]{2,1,0:T(8,128)S(1)} %get-tuple-element.56), channel_id=1, source_target_pairs={{0,1},{1,2},{2,3},{4,5},{5,6},{6,7},{8,9},{9,10},{10,11},{12,13},{... | collective-permute-start | bytes 49160 | tf_op jit(solution)/shard_map/ppermute | solution.py:268
  46.5 4.3 %collective-permute-start.7 = (f32[1,32,128]{2,1,0:T(8,128)S(1)}, f32[1,32,128]{2,1,0:T(8,128)S(1)}, u32[]{:S(2)}, u32[]{:S(2)}) collective-permute-start(f32[1,32,128]{2,1,0:T(8,128)S(1)} %get-tuple-element.57), channel_id=1, source_target_pairs={{1,0},{2,1},{3,2},{5,4},{6,5},{7,6},{9,8},{10,9},{11,10},{13,12},{... | collective-permute-start | bytes 49160 | tf_op jit(solution)/shard_map/ppermute | solution.py:268

commit v3 on v2

--- a/solution.py
+++ b/solution.py
@@ -37,14 +37,16 @@
     return -(-count // LANES)
 
 
-def to_scalars(column, staged, scalars):
+def to_scalars(column, staged, scalars, sem):
     count = column.shape[0]
     for j in range(scalar_rows(count)):
         part = column[j * LANES : (j + 1) * LANES]
         shape = (part.shape[0], LANES)
         own = lax.broadcasted_iota(jnp.int32, shape, 0) == lax.broadcasted_iota(jnp.int32, shape, 1)
         staged[j : j + 1, :] = jnp.sum(jnp.where(own, part, 0), axis=0, keepdims=True)
-    pltpu.sync_copy(staged, scalars)
+    copy = pltpu.make_async_copy(staged, scalars, sem)
+    copy.start()
+    return copy
 
 
 def scalar_at(scalars, index):
@@ -85,7 +87,7 @@
         for r in range(columns // LANES):
             before = before + (block[r : r + 1, :] < owner_row).astype(jnp.int32)
         before = jnp.sum(before.astype(jnp.float32), axis=1, keepdims=True)
-        to_scalars(before.astype(jnp.int32), staged, starts)
+        bounds_copy = to_scalars(before.astype(jnp.int32), staged, starts, sems.at[6])
         for copy in copies[1:]:
             copy.wait()
 
@@ -103,6 +105,7 @@
             return carry
 
         lax.fori_loop(0, columns // LANES, flux, 0, unroll=16)
+        bounds_copy.wait()
         lane = lax.broadcasted_iota(jnp.int32, (1, LANES), 1)
 
         def window(owner, carry):
@@ -152,7 +155,7 @@
             pltpu.VMEM(root.shape, jnp.float32),
             pltpu.VMEM(root.shape, jnp.float32),
             pltpu.VMEM((bounds, LANES), jnp.int32),
-            pltpu.SemaphoreType.DMA((6,)),
+            pltpu.SemaphoreType.DMA((7,)),
         ],
         compiler_params=params(),
         name="dispatch",
@@ -171,23 +174,21 @@
     )
 
 
-def scatter_kernel(layers, cells_x, cells_y, batch):
+def scatter_kernel(layers, cells_x, cells_y, devices, batch):
     fields = layers + 1
     half = layers * cells_x
 
-    def kernel(incoming, mask, out, low, high, order, total, spread, staged, used):
+    def kernel(incoming, mask, out, low, high, order, total, spread, staged, used, sem):
         chunks = incoming.shape[0] // fields
         first_cells = incoming[pl.ds(layers, chunks, stride=fields), :][:, 0:1]
-        to_scalars((first_cells >= 0.0).astype(jnp.int32), staged, used)
-
-        def listed(c, filled):
-            holds = scalar_at(used, c)
-            order[jnp.where(holds > 0, filled, chunks - 1 - (c - filled))] = c
-            return filled + holds
-
-        filled = lax.fori_loop(0, chunks, listed, 0, unroll=8)
-        batches = (filled + batch - 1) // batch
-        order[chunks] = filled
+        used_copy = to_scalars((first_cells >= 0.0).astype(jnp.int32), staged, used, sem)
+        each = chunks // devices
+
+        def first(sender, carry):
+            order[sender] = sender * each
+            return carry
+
+        lax.fori_loop(0, devices, first, 0, unroll=8)
         total[...] = jnp.zeros_like(total)
         row_x = lax.broadcasted_iota(jnp.int32, (cells_x, LANES), 0)
         row_y = lax.broadcasted_iota(jnp.int32, (cells_y, LANES), 0)
@@ -222,7 +223,20 @@
             )
             return carry
 
-        lax.fori_loop(0, batches, step, 0)
+        lax.fori_loop(0, devices // batch, step, 0)
+        used_copy.wait()
+
+        def listed(r, filled):
+            c = r // (each - 1) * each + 1 + r % (each - 1)
+            holds = scalar_at(used, c)
+            order[jnp.where(holds > 0, filled, chunks - 1 - (r - (filled - devices)))] = c
+            return filled + holds
+
+        filled = jnp.int32(devices)
+        if each > 1:
+            filled = lax.fori_loop(0, chunks - devices, listed, filled, unroll=8)
+        order[chunks] = filled
+        lax.fori_loop(devices // batch, (filled + batch - 1) // batch, step, 0)
         land = mask[...].astype(jnp.float32)
         for k in range(layers):
             rows = slice(k * cells_x, (k + 1) * cells_x)
@@ -235,13 +249,13 @@
     return kernel
 
 
-def scatter(incoming, mask, layers, cells_x, cells_y):
+def scatter(incoming, mask, layers, cells_x, cells_y, devices):
     chunks = incoming.shape[0] // (layers + 1)
-    batch = max(b for b in (8, 6, 4, 3, 2, 1) if chunks % b == 0)
+    batch = max(b for b in (8, 4, 2, 1) if devices % b == 0)
     strip = jax.ShapeDtypeStruct((layers, HALO, cells_y), jnp.float32)
     vmem = pl.BlockSpec(memory_space=pltpu.VMEM)
     return pl.pallas_call(
-        scatter_kernel(layers, cells_x, cells_y, batch),
+        scatter_kernel(layers, cells_x, cells_y, devices, batch),
         out_shape=(
             jax.ShapeDtypeStruct((layers, cells_x, cells_y), jnp.float32),
             strip,
@@ -255,6 +269,7 @@
             pltpu.VMEM((2 * layers * cells_x, batch * LANES), jnp.bfloat16),
             pltpu.VMEM((scalar_rows(chunks), LANES), jnp.int32),
             pltpu.SMEM((scalar_rows(chunks), LANES), jnp.int32),
+            pltpu.SemaphoreType.DMA(()),
         ],
         compiler_params=params(),
         name="scatter",
@@ -641,7 +656,7 @@
 
 def newton(begun, source, incoming, order, layers, cells_x, cells_y):
     grid = Stencil(layers, cells_x, cells_y)
-    turned = 5
+    turned = 2 * layers // 5
     chunks = incoming.shape[0] // (layers + 1)
     shape = (layers, grid.high_x, grid.wide)
     field = pltpu.VMEM(shape, jnp.float32)
@@ -737,7 +752,7 @@
     fixed = (fixed, below, above, side_left, side_right)
     incoming = flat.reshape(outgoing.shape)
 
-    source, low, high, order = scatter(incoming, land_mask, layers, cells_x, cells_y)
+    source, low, high, order = scatter(incoming, land_mask, layers, cells_x, cells_y, devices)
     below, above = both_ways(low, high, "gx")
     begun = begin(fixed, layers, cells_x, cells_y)
     source, below, above = source[None], below[None], above[None]

time: 86.4 us -> 85.6 us (level)
  no operation moved by 1% of the time
where the time goes in v3:
time: 85.6 us; the launch traced here: 85.2 us
  Pallas kernels  26.2 us (31%)
  starting transfers between devices  23.2 us (27%)
  blocking collectives  22.1 us (26%)
  waiting for transfers between devices  12.8 us (15%)
  between operations  0.87 us (1%)
    all_to_all x1, blocking collectives, on_device(): lax.all_to_all(reply.reshape(-1), axes, split_axis=0, concat_axis=0, tile...  22.1 us
    all_to_all x1, waiting for transfers between devices, on_device(): lax.all_to_all(outgoing.reshape(-1), axes, split_axis=0, concat_axis=0, t...  10.7 us
    ppermute x4, starting transfers between devices, both_ways(): lax.ppermute(high_end, axis, forward)  10.7 us
    pallas_call x1, Pallas kernels, newton(): pl.pallas_call(newton_kernel(grid, turned), out_shape=(jax.ShapeDtypeStru...  10.6 us
    all_to_all x1, starting transfers between devices, on_device(): lax.all_to_all(outgoing.reshape(-1), axes, split_axis=0, concat_axis=0, t...  7.33 us
    pallas_call x1, Pallas kernels, scatter(): pl.pallas_call(scatter_kernel(layers, cells_x, cells_y, devices, batch),...  6.45 us
    ppermute x4, starting transfers between devices, both_ways(): lax.ppermute(low_end, axis, backward)  5.17 us
    pallas_call x1, Pallas kernels, dispatch(): pl.pallas_call(dispatch_kernel(layers, devices, capacity), out_shape=(jax...  3.48 us
  transfers between devices with their start and end apart: 9, of which 3 were waited for; matrix products, arithmetic and copies ran while one was open for 0% of the time, Pallas kernels for 12%

profile of v3, /device:TPU:0, one launch (start us, length us, event | category | flops | bytes accessed | tf_op | source)
XLA Modules:
  0.0 85.2 jit_solution(3141636462816445322)
XLA Ops:
  0.6 0.0 copy-start.3
  0.6 3.5 %dispatch.1 = (f32[1056,128]{1,0:T(8,128)}, s32[1,128]{1,0:T(1,128)S(1)}) custom-call(s32[64,128]{1,0:T(8,128)} %bitcast.21, s32[64,128]{1,0:T(8,128)} %bitcast.22, f32[64,128]{1,0:T(8,128)} %bitcast.23, f32[64,128]{1,0:T(8,128)} %bitcast.24, f32[10,8192]{1,0:T(8,128)} %root_hbm.1, f32[10,8192]{1,0:T(8,128)} %sat_hbm.1), custom_call_target="tpu_custom_call" | custom-call | tf_op jit(solution)/shard_map/dispatch/pallas_call | solution.py:141
  4.1 0.0 copy-start
  4.1 0.0 copy-start.1
  4.2 0.0 copy-start.2
  4.2 7.3 %all-to-all-start = ((f32[32,4224,1]{1,2,0:T(1,128)}), f32[32,4224,1]{1,2,0:T(1,128)S(1)}, u32[]{:S(2)}, u32[]{:S(2)}) async-start(f32[32,4224,1]{1,2,0:T(1,128)} %bitcast.4), calls=%async_computation | async-start | bytes 1081344 | tf_op jit(solution)/shard_map/all_to_all | solution.py:746
  11.5 0.0 copy-done.3
  11.5 0.0 copy-done
  11.5 0.0 copy-done.1
  11.5 0.0 copy-done.2
  11.5 0.0 copy-start.4
  11.6 0.1 prepare.1
  11.7 3.7 %collective-permute-start = (f32[3,10,8,256]{3,2,1,0:T(8,128)S(1)}, f32[3,10,8,256]{3,2,1,0:T(8,128)S(1)}, u32[]{:S(2)}, u32[]{:S(2)}) collective-permute-start(f32[3,10,8,256]{3,2,1,0:T(8,128)S(1)} %get-tuple-element.33), channel_id=1, source_target_pairs={{0,4},{4,8},{8,12},{12,16},{16,20},{20,24},{24,28},{1,5},{5,9},{9,... | collective-permute-start | bytes 737288 | tf_op jit(solution)/shard_map/ppermute | solution.py:283
  15.4 1.3 %collective-permute-start.1 = (f32[3,10,8,256]{3,2,1,0:T(8,128)S(1)}, f32[3,10,8,256]{3,2,1,0:T(8,128)S(1)}, u32[]{:S(2)}, u32[]{:S(2)}) collective-permute-start(f32[3,10,8,256]{3,2,1,0:T(8,128)S(1)} %get-tuple-element.34), channel_id=1, source_target_pairs={{4,0},{8,4},{12,8},{16,12},{20,16},{24,20},{28,24},{5,1},{9,5},{13... | collective-permute-start | bytes 737288 | tf_op jit(solution)/shard_map/ppermute | solution.py:283
  16.7 10.7 %all-to-all-done = f32[32,4224,1]{1,2,0:T(1,128)S(1)} async-done(((f32[32,4224,1]{1,2,0:T(1,128)}), f32[32,4224,1]{1,2,0:T(1,128)S(1)}, u32[]{:S(2)}, u32[]{:S(2)}) %all-to-all-start) | async-done | bytes 540704 | tf_op jit(solution)/shard_map/all_to_all | solution.py:746
  27.4 0.0 copy-done.4
  27.4 6.5 %scatter.1 = (f32[10,32,256]{2,1,0:T(8,128)S(1)}, f32[10,8,256]{2,1,0:T(8,128)S(1)}, f32[10,8,256]{2,1,0:T(8,128)S(1)}, s32[97]{0:T(128)S(1)}) custom-call(f32[1056,128]{1,0:T(8,128)S(1)} %bitcast.11, s32[32,256]{1,0:T(8,128)S(1)} %copy-done.4), custom_call_target="tpu_custom_call" | custom-call | tf_op jit(solution)/shard_map/scatter/pallas_call | solution.py:257
  33.9 3.3 %collective-permute-start.4 = (f32[10,8,256]{2,1,0:T(8,128)S(1)}, f32[10,8,256]{2,1,0:T(8,128)S(1)}, u32[]{:S(2)}, u32[]{:S(2)}) collective-permute-start(f32[10,8,256]{2,1,0:T(8,128)S(1)} %get-tuple-element.54), channel_id=1, source_target_pairs={{0,4},{4,8},{8,12},{12,16},{16,20},{20,24},{24,28},{1,5},{5,9},{9,... | collective-permute-start | bytes 245768 | tf_op jit(solution)/shard_map/ppermute | solution.py:283
  37.2 1.3 %collective-permute-start.5 = (f32[10,8,256]{2,1,0:T(8,128)S(1)}, f32[10,8,256]{2,1,0:T(8,128)S(1)}, u32[]{:S(2)}, u32[]{:S(2)}) collective-permute-start(f32[10,8,256]{2,1,0:T(8,128)S(1)} %get-tuple-element.55), channel_id=1, source_target_pairs={{4,0},{8,4},{12,8},{16,12},{20,16},{24,20},{28,24},{5,1},{9,5},{13... | collective-permute-start | bytes 245768 | tf_op jit(solution)/shard_map/ppermute | solution.py:283
  38.5 0.0 collective-permute-done.below.low
  38.5 0.0 collective-permute-done.1.above.high
  38.5 0.4 pack.2
  38.9 1.5 %collective-permute-start.2 = (f32[3,32,128]{2,1,0:T(8,128)S(1)}, f32[3,32,128]{2,1,0:T(8,128)S(1)}, u32[]{:S(2)}, u32[]{:S(2)}) collective-permute-start(f32[3,32,128]{2,1,0:T(8,128)S(1)} %get-tuple-element.35), channel_id=1, source_target_pairs={{0,1},{1,2},{2,3},{4,5},{5,6},{6,7},{8,9},{9,10},{10,11},{12,13},{... | collective-permute-start | bytes 147464 | tf_op jit(solution)/shard_map/ppermute | solution.py:283
  40.4 1.3 %collective-permute-start.3 = (f32[3,32,128]{2,1,0:T(8,128)S(1)}, f32[3,32,128]{2,1,0:T(8,128)S(1)}, u32[]{:S(2)}, u32[]{:S(2)}) collective-permute-start(f32[3,32,128]{2,1,0:T(8,128)S(1)} %get-tuple-element.36), channel_id=1, source_target_pairs={{1,0},{2,1},{3,2},{5,4},{6,5},{7,6},{9,8},{10,9},{11,10},{13,12},{... | collective-permute-start | bytes 147464 | tf_op jit(solution)/shard_map/ppermute | solution.py:283
  41.7 0.0 collective-permute-done.4
  41.7 1.8 %collective-permute-done.5 = f32[10,8,256]{2,1,0:T(8,128)S(1)} collective-permute-done((f32[10,8,256]{2,1,0:T(8,128)S(1)}, f32[10,8,256]{2,1,0:T(8,128)S(1)}, u32[]{:S(2)}, u32[]{:S(2)}) %collective-permute-start.5) | collective-permute-done | bytes 81952 | tf_op jit(solution)/shard_map/ppermute | solution.py:283
  43.5 0.2 pack.3
  43.7 2.3 %collective-permute-start.6 = (f32[1,32,128]{2,1,0:T(8,128)S(1)}, f32[1,32,128]{2,1,0:T(8,128)S(1)}, u32[]{:S(2)}, u32[]{:S(2)}) collective-permute-start(f32[1,32,128]{2,1,0:T(8,128)S(1)} %get-tuple-element.56), channel_id=1, source_target_pairs={{0,1},{1,2},{2,3},{4,5},{5,6},{6,7},{8,9},{9,10},{10,11},{12,13},{... | collective-permute-start | bytes 49160 | tf_op jit(solution)/shard_map/ppermute | solution.py:283
  46.0 1.3 %collective-permute-start.7 = (f32[1,32,128]{2,1,0:T(8,128)S(1)}, f32[1,32,128]{2,1,0:T(8,128)S(1)}, u32[]{:S(2)}, u32[]{:S(2)}) collective-permute-start(f32[1,32,128]{2,1,0:T(8,128)S(1)} %get-tuple-element.57), channel_id=1, source_target_pairs={{1,0},{2,1},{3,2},{5,4},{6,5},{7,6},{9,8},{10,9},{11,10},{13,12},{... | collective-permute-start | bytes 49160 | tf_op jit(solution)/shard_map/ppermute | solution.py:283
  47.3 0.0 collective-permute-done.2.side_left
  47.3 0.0 collective-permute-done.3.side_right
  47.3 2.8 %begin.1 = (f32[10,48,384]{2,1,0:T(8,128)S(1)}, f32[10,48,384]{2,1,0:T(8,128)S(1)}, f32[10,48,384]{2,1,0:T(8,128)S(1)}, f32[48,384]{1,0:T(8,128)S(1)}, f32[10,48...) custom-call(f32[3,10,32,256]{3,2,1,0:T(8,128)S(1)} %get-tuple-elemen, ...), custom_call_target="tpu_custom_call" | custom-call | flops 18432000 | tf_op jit(solution)/shard_map/begin/pallas_call | solution.py:591
  50.1 0.0 collective-permute-done.6.src_left
  50.1 0.2 collective-permute-done.7.src_right
  50.3 10.6 %newton.1 = (f32[10,32,256]{2,1,0:T(8,128)}, f32[960,128]{1,0:T(8,128)S(1)}) custom-call(f32[10,48,384]{2,1,0:T(8,128)S(1)} %get-tuple-element.37.pres0, f32[10,48,384]{2,1,0:T(8,128)S(1)} %get-tuple-element.38.poro, f32[10,48,384]{2,1,0:T(8,128)S(1)} %get-tuple-element.39.stored, f32[48,384]{1,0:T(8,128)S(1)} %get-tuple-element.40.last_perm, ...), custom_call_target="tpu_custom_call" | custom-call | tf_op jit(solution)/shard_map/newton/pallas_call | solution.py:665
  60.9 22.1 %all_to_all.18 = f32[32,3840,1]{1,2,0:T(1,128)S(1)} all-to-all(f32[32,3840,1]{1,2,0:T(1,128)S(1)} %bitcast.16), channel_id=1, replica_groups=mesh['gx'=8,'gy'=4] {'gx','gy'}, dimensions={0} | all-to-all | bytes 983040 | tf_op jit(solution)/shard_map/all_to_all | solution.py:764
  83.0 2.2 %combine.1 = f32[10,8192]{1,0:T(8,128)} custom-call(s32[1,128]{1,0:T(1,128)S(1)} %get-tuple-element.60.starts, f32[960,128]{1,0:T(8,128)S(1)} %bitcast.13), custom_call_target="tpu_custom_call" | custom-call | tf_op jit(solution)/shard_map/combine/pallas_call | solution.py:713
Async XLA Ops:
  0.6 10.9 %copy-start.3 = (f32[10,32,256]{2,1,0:T(8,128)S(1)}, f32[10,32,256]{2,1,0:T(8,128)}, u32[]{:S(2)}) copy-start(f32[10,32,256]{2,1,0:T(8,128)} %pressure.1) | copy-start | bytes 983044
  4.1 7.4 %copy-start = (f32[10,32,256]{2,1,0:T(8,128)S(1)}, f32[10,32,256]{2,1,0:T(8,128)}, u32[]{:S(2)}) copy-start(f32[10,32,256]{2,1,0:T(8,128)} %conductivity.1) | copy-start | bytes 983044
  4.1 7.4 %copy-start.1 = (s32[10,32,256]{2,1,0:T(8,128)S(1)}, s32[10,32,256]{2,1,0:T(8,128)}, u32[]{:S(2)}) copy-start(s32[10,32,256]{2,1,0:T(8,128)} %freeze.1) | copy-start | bytes 983044
  4.2 7.4 %copy-start.2 = (f32[10,32,256]{2,1,0:T(8,128)S(1)}, f32[10,32,256]{2,1,0:T(8,128)}, u32[]{:S(2)}) copy-start(f32[10,32,256]{2,1,0:T(8,128)} %porosity.1) | copy-start | bytes 983044
  4.2 23.3 %all-to-all-start = ((f32[32,4224,1]{1,2,0:T(1,128)}), f32[32,4224,1]{1,2,0:T(1,128)S(1)}, u32[]{:S(2)}, u32[]{:S(2)}) async-start(f32[32,4224,1]{1,2,0:T(1,128)} %bitcast.4), calls=%async_computation | async-start | bytes 1081344 | tf_op jit(solution)/shard_map/all_to_all | solution.py:746
  11.5 15.9 %copy-start.4 = (s32[32,256]{1,0:T(8,128)S(1)}, s32[32,256]{1,0:T(8,128)}, u32[]{:S(2)}) copy-start(s32[32,256]{1,0:T(8,128)} %mask.1) | copy-start | bytes 98308
  11.7 26.8 %collective-permute-start = (f32[3,10,8,256]{3,2,1,0:T(8,128)S(1)}, f32[3,10,8,256]{3,2,1,0:T(8,128)S(1)}, u32[]{:S(2)}, u32[]{:S(2)}) collective-permute-start(f32[3,10,8,256]{3,2,1,0:T(8,128)S(1)} %get-tuple-element.33), channel_id=1, source_target_pairs={{0,4},{4,8},{8,12},{12,16},{16,20},{20,24},{24,28},{1,5},{5,9},{9,... | collective-permute-start | bytes 737288 | tf_op jit(solution)/shard_map/ppermute | solution.py:283
  15.4 23.1 %collective-permute-start.1 = (f32[3,10,8,256]{3,2,1,0:T(8,128)S(1)}, f32[3,10,8,256]{3,2,1,0:T(8,128)S(1)}, u32[]{:S(2)}, u32[]{:S(2)}) collective-permute-start(f32[3,10,8,256]{3,2,1,0:T(8,128)S(1)} %get-tuple-element.34), channel_id=1, source_target_pairs={{4,0},{8,4},{12,8},{16,12},{20,16},{24,20},{28,24},{5,1},{9,5},{13... | collective-permute-start | bytes 737288 | tf_op jit(solution)/shard_map/ppermute | solution.py:283
  33.9 7.8 %collective-permute-start.4 = (f32[10,8,256]{2,1,0:T(8,128)S(1)}, f32[10,8,256]{2,1,0:T(8,128)S(1)}, u32[]{:S(2)}, u32[]{:S(2)}) collective-permute-start(f32[10,8,256]{2,1,0:T(8,128)S(1)} %get-tuple-element.54), channel_id=1, source_target_pairs={{0,4},{4,8},{8,12},{12,16},{16,20},{20,24},{24,28},{1,5},{5,9},{9,... | collective-permute-start | bytes 245768 | tf_op jit(solution)/shard_map/ppermute | solution.py:283
  37.2 6.3 %collective-permute-start.5 = (f32[10,8,256]{2,1,0:T(8,128)S(1)}, f32[10,8,256]{2,1,0:T(8,128)S(1)}, u32[]{:S(2)}, u32[]{:S(2)}) collective-permute-start(f32[10,8,256]{2,1,0:T(8,128)S(1)} %get-tuple-element.55), channel_id=1, source_target_pairs={{4,0},{8,4},{12,8},{16,12},{20,16},{24,20},{28,24},{5,1},{9,5},{13... | collective-permute-start | bytes 245768 | tf_op jit(solution)/shard_map/ppermute | solution.py:283
  38.9 8.4 %collective-permute-start.2 = (f32[3,32,128]{2,1,0:T(8,128)S(1)}, f32[3,32,128]{2,1,0:T(8,128)S(1)}, u32[]{:S(2)}, u32[]{:S(2)}) collective-permute-start(f32[3,32,128]{2,1,0:T(8,128)S(1)} %get-tuple-element.35), channel_id=1, source_target_pairs={{0,1},{1,2},{2,3},{4,5},{5,6},{6,7},{8,9},{9,10},{10,11},{12,13},{... | collective-permute-start | bytes 147464 | tf_op jit(solution)/shard_map/ppermute | solution.py:283
  40.4 6.9 %collective-permute-start.3 = (f32[3,32,128]{2,1,0:T(8,128)S(1)}, f32[3,32,128]{2,1,0:T(8,128)S(1)}, u32[]{:S(2)}, u32[]{:S(2)}) collective-permute-start(f32[3,32,128]{2,1,0:T(8,128)S(1)} %get-tuple-element.36), channel_id=1, source_target_pairs={{1,0},{2,1},{3,2},{5,4},{6,5},{7,6},{9,8},{10,9},{11,10},{13,12},{... | collective-permute-start | bytes 147464 | tf_op jit(solution)/shard_map/ppermute | solution.py:283
  43.7 6.4 %collective-permute-start.6 = (f32[1,32,128]{2,1,0:T(8,128)S(1)}, f32[1,32,128]{2,1,0:T(8,128)S(1)}, u32[]{:S(2)}, u32[]{:S(2)}) collective-permute-start(f32[1,32,128]{2,1,0:T(8,128)S(1)} %get-tuple-element.56), channel_id=1, source_target_pairs={{0,1},{1,2},{2,3},{4,5},{5,6},{6,7},{8,9},{9,10},{10,11},{12,13},{... | collective-permute-start | bytes 49160 | tf_op jit(solution)/shard_map/ppermute | solution.py:283
  46.0 4.3 %collective-permute-start.7 = (f32[1,32,128]{2,1,0:T(8,128)S(1)}, f32[1,32,128]{2,1,0:T(8,128)S(1)}, u32[]{:S(2)}, u32[]{:S(2)}) collective-permute-start(f32[1,32,128]{2,1,0:T(8,128)S(1)} %get-tuple-element.57), channel_id=1, source_target_pairs={{1,0},{2,1},{3,2},{5,4},{6,5},{7,6},{9,8},{10,9},{11,10},{13,12},{... | collective-permute-start | bytes 49160 | tf_op jit(solution)/shard_map/ppermute | solution.py:283
